TPU v7x, 8 devices: a whole 2x2x1 slice. The times are simulated.
8 devices in a mesh: dp: 1 (over z), sp: 8 (over y, x, core).
Axes of the slice: x: 2, y: 2, z: 1, core: 2. Of those that a mesh axis runs over, the one named last changes fastest.
Arguments:
- dec_hidden: bfloat16 [2048, 4096], P(('dp', 'sp'))
- enc_memory: bfloat16 [8192, 4096], P(('dp', 'sp'))
- mem_len: int32 [1], P('dp')
- norm_self: bfloat16 [2, 4096], replicated
- norm_cross: bfloat16 [2, 4096], replicated
- norm_mlp: bfloat16 [2, 4096], replicated
- self_q: bfloat16 [2, 4096, 4096], replicated
- self_k: bfloat16 [2, 4096, 4096], replicated
- self_v: bfloat16 [2, 4096, 4096], replicated
- self_o: bfloat16 [2, 32, 128, 4096], replicated
- cross_q: bfloat16 [2, 4096, 4096], replicated
- cross_k: bfloat16 [2, 4096, 1024], replicated
- cross_v: bfloat16 [2, 4096, 1024], replicated
- cross_o: bfloat16 [2, 32, 128, 4096], replicated
- mlp_gate: bfloat16 [2, 4096, 14336], replicated
- mlp_up: bfloat16 [2, 4096, 14336], replicated
- mlp_down: bfloat16 [2, 14336, 4096], replicated
Outputs:
- output: bfloat16 [2048, 4096], P(('dp', 'sp'))
All inputs are finite; a program needn't handle non-finite values.
Results may differ from a plain program's by a relative error of at most 0.0127063.
Values are sent between devices in bfloat16 or wider.
A program may use at most 4.5 GiB of HBM per device.

v0:
```python
import jax
import jax.numpy as jnp
from jax import lax
from jax.sharding import PartitionSpec as P

EPS = 1e-6
NEG_BIG = -1e30


def rms_norm(hidden, gain_vec):
    hidden32 = hidden.astype(jnp.float32)
    inv_rms = lax.rsqrt(jnp.mean(hidden32 * hidden32, axis=-1, keepdims=True) + EPS)
    return (hidden32 * inv_rms * gain_vec.astype(jnp.float32)).astype(jnp.bfloat16)


def project(acts, weight_mat):
    return jnp.dot(acts, weight_mat, preferred_element_type=jnp.float32).astype(jnp.bfloat16)


def add_residual(hidden, update):
    return (hidden.astype(jnp.float32) + update).astype(jnp.bfloat16)


def solution(mesh):
    group = mesh.shape['sp']
    row_spec = P(('dp', 'sp'), None)

    def local_step(hidden, memory, mem_len, norm_self, norm_cross, norm_mlp, self_q, self_k, self_v, self_o, cross_q, cross_k, cross_v, cross_o, mlp_gate, mlp_up, mlp_down):
        rows, width = hidden.shape
        mem_rows = memory.shape[0]
        n_heads, head_dim = self_o.shape[1], self_o.shape[2]
        kv_heads = cross_k.shape[2] // head_dim
        n_groups = n_heads // kv_heads
        all_rows = rows * group
        soft_scale = head_dim ** -0.5
        shard_index = lax.axis_index('sp')
        query_pos = shard_index * rows + jnp.arange(rows)
        causal = query_pos[:, None] >= jnp.arange(all_rows)[None, :]
        mem_valid = (shard_index * mem_rows + jnp.arange(mem_rows)) < mem_len[0]
        for layer in range(norm_self.shape[0]):
            normed = rms_norm(hidden, norm_self[layer])
            queries = project(normed, self_q[layer]).reshape(rows, n_heads, head_dim)
            keys_all = lax.all_gather(project(normed, self_k[layer]), 'sp', axis=0, tiled=True).reshape(all_rows, n_heads, head_dim)
            values_all = lax.all_gather(project(normed, self_v[layer]), 'sp', axis=0, tiled=True).reshape(all_rows, n_heads, head_dim)
            scores = jnp.einsum('thd,shd->hts', queries, keys_all, preferred_element_type=jnp.float32) * soft_scale
            scores = jnp.where(causal, scores, NEG_BIG)
            weights = jnp.exp(scores - jnp.max(scores, axis=-1, keepdims=True))
            numerator = jnp.einsum('hts,shd->htd', weights.astype(jnp.bfloat16), values_all, preferred_element_type=jnp.float32)
            attended = (numerator / jnp.sum(weights, axis=-1, keepdims=True)).astype(jnp.bfloat16)
            hidden = add_residual(hidden, jnp.einsum('htd,hdo->to', attended, self_o[layer], preferred_element_type=jnp.float32))

            normed = rms_norm(hidden, norm_cross[layer])
            cross_queries = lax.all_gather(project(normed, cross_q[layer]), 'sp', axis=0, tiled=True).reshape(all_rows, kv_heads, n_groups, head_dim)
            mem_keys = project(memory, cross_k[layer]).reshape(mem_rows, kv_heads, head_dim)
            mem_values = project(memory, cross_v[layer]).reshape(mem_rows, kv_heads, head_dim)
            scores = jnp.einsum('tkgd,skd->kgts', cross_queries, mem_keys, preferred_element_type=jnp.float32) * soft_scale
            scores = jnp.where(mem_valid, scores, NEG_BIG)
            part_max = jnp.max(scores, axis=-1, keepdims=True)
            weights = jnp.exp(scores - part_max)
            part_sum = jnp.sum(weights, axis=-1, keepdims=True)
            part_num = jnp.einsum('kgts,skd->kgtd', weights.astype(jnp.bfloat16), mem_values, preferred_element_type=jnp.float32)
            rescale = jnp.exp(part_max - lax.pmax(part_max, 'sp'))
            packed = jnp.concatenate([part_num * rescale, part_sum * rescale], axis=-1)
            combined = lax.psum_scatter(packed, 'sp', scatter_dimension=2, tiled=True)
            attended = (combined[..., :head_dim] / combined[..., head_dim:]).astype(jnp.bfloat16)
            out_heads = cross_o[layer].reshape(kv_heads, n_groups, head_dim, width)
            hidden = add_residual(hidden, jnp.einsum('kgtd,kgdo->to', attended, out_heads, preferred_element_type=jnp.float32))

            normed = rms_norm(hidden, norm_mlp[layer])
            gate_pre = jnp.dot(normed, mlp_gate[layer], preferred_element_type=jnp.float32)
            up_proj = jnp.dot(normed, mlp_up[layer], preferred_element_type=jnp.float32)
            hidden_act = (jax.nn.silu(gate_pre) * up_proj).astype(jnp.bfloat16)
            hidden = add_residual(hidden, jnp.dot(hidden_act, mlp_down[layer], preferred_element_type=jnp.float32))
        return hidden

    return jax.shard_map(local_step, mesh=mesh, in_specs=(row_spec, row_spec, P('dp')) + (P(),) * 14, out_specs=row_spec, check_vma=False)
```

profile of v0, /device:TPU:0, one launch (start us, length us, event | category | flops | bytes accessed | tf_op | source)
XLA Modules:
  0.0 2088.8 jit_solution(1649804483092247262)
XLA Ops:
  6.5 1.4 slice_convert_fusion.2
  8.0 2.1 fusion.210
  10.1 16.8 fusion.179
  26.9 0.0 all-gather.9.cloned.1.call-start
  27.0 16.1 fusion.182
  43.1 0.3 all-gather.11.cloned.1.call-start
  43.5 0.4 iota_compare_fusion
  43.9 0.7 slice_convert_fusion.1
  44.6 15.7 fusion.293
  60.3 53.7 %all-gather.7.cloned.1.call-done = bf16[2048,4096]{1,0:T(8,128)(2,1)} async-done(((bf16[256,4096]{1,0:T(8,128)(2,1)}), bf16[2048,4096]{1,0:T(8,128)(2,1)}) %all-gather.7.cloned.1.call-update) | async-done | bytes 16777232 | tf_op jit(solution)/shard_map/all_gather | solution.py:43
  114.0 29.9 %fusion.30 = (f32[32,256]{1,0:T(8,128)S(1)}, f32[32,256,2048]{2,1,0:T(8,128)}) fusion(pred[256,2048]{1,0:T(8,128)(4,1)S(1)} %iota_compare_fusion, bf16[32,32,8,128]{3,2,1,0:T(8,128)(2,1)S(1)} %fusion.293, bf16[2048,4096]{1,0:T(8,128)(2,1)} %all-gather.7.cloned.1.call-done), kind=kOutput, calls=%fused_computation.38 | convolution fusion | flops 4345290752 | bytes 86540288 | tf_op jit(solution)/shard_map/thd,shd->hts/dot_general | solution.py:45
  143.9 21.5 %fusion.32 = f32[32,256]{1,0:T(8,128)S(1)} fusion(f32[32,256,2048]{2,1,0:T(8,128)} %get-tuple-element.18, f32[32,256]{1,0:T(8,128)S(1)} %get-tuple-element.17, pred[256,2048]{1,0:T(8,128)(4,1)S(1)} %iota_compare_fusion), kind=kLoop, calls=%fused_computation.40 | loop fusion | flops 67100672 | bytes 67698688 | tf_op jit(solution)/shard_map/reduce_sum | solution.py:49
  165.4 34.5 %all-gather.9.cloned.1.call-done = bf16[2048,4096]{1,0:T(8,128)(2,1)} async-done(((bf16[256,4096]{1,0:T(8,128)(2,1)}), bf16[2048,4096]{1,0:T(8,128)(2,1)}) %all-gather.9.cloned.1.call-update) | async-done | bytes 16777232 | tf_op jit(solution)/shard_map/all_gather | solution.py:44
  199.9 31.7 %divide_convert_fusion.2.clone.5 = bf16[32,256,128]{2,1,0:T(8,128)(2,1)} fusion(f32[32,256,2048]{2,1,0:T(8,128)} %get-tuple-element.18, f32[32,256]{1,0:T(8,128)S(1)} %get-tuple-element.17, pred[256,2048]{1,0:T(8,128)(4,1)S(1)} %iota_compare_fusion, f32[32,256]{1,0:T(8,128)S(1)} %fusion.32, ...), kind=kOutput, calls=%fused_computation.187.clone.clone.clone.clone.2 | convolution fusion | flops 4364173312 | bytes 86573056 | tf_op jit(solution)/shard_map/hts,shd->htd/dot_general | solution.py:48
  231.6 16.0 fusion.213
  247.6 16.7 fusion.185
  265.0 13.9 fusion.278
  278.9 14.8 fusion.281
  293.7 54.8 %all-gather.11.cloned.1.call-done = bf16[2048,4096]{1,0:T(8,128)(2,1)} async-done(((bf16[256,4096]{1,0:T(8,128)(2,1)}), bf16[2048,4096]{1,0:T(8,128)(2,1)}) %all-gather.11.cloned.1.call-update) | async-done | bytes 16777232 | tf_op jit(solution)/shard_map/all_gather | solution.py:53
  348.5 27.4 %reshape.98 = bf16[2048,8,4,128]{3,2,1,0:T(4,128)(2,1)} reshape(bf16[2048,4096]{1,0:T(8,128)(2,1)} %all-gather.11.cloned.1.call-done) | data formatting | bytes 33554432 | tf_op jit(solution)/shard_map/reshape | solution.py:53
  375.8 94.7 %bitcast_reduce_fusion.1 = (f32[8,4,2048]{2,1,0:T(4,128)S(1)}, f32[8,1024,2048,4]{2,1,3,0:T(8,128)}) fusion(pred[1024]{0:T(1024)(128)(4,1)S(1)} %add_compare_fusion, bf16[1024,8,128,1]{0,2,3,1:T(8,128)(2,1)S(1)} %bitcast.342, bf16[2048,8,4,128]{3,2,1,0:T(4,128)(2,1)} %reshape.98), kind=kOutput, calls=%fused_computation.4 | convolution fusion | flops 17381130240 | bytes 287572992 | tf_op jit(solution)/shard_map/tkgd,skd->kgts/dot_general | solution.py:56
  470.5 0.9 broadcast_in_dim.54
  471.5 80.9 %fusion.2 = f32[8,4,2048]{2,1,0:T(4,128)S(1)} fusion(f32[8,1024,2048,4]{2,1,3,0:T(8,128)} %get-tuple-element.22, f32[8,4,2048]{2,1,0:T(4,128)S(1)} %get-tuple-element.21, pred[1024]{0:T(1024)(128)(4,1)S(1)} %add_compare_fusion), kind=kLoop, calls=%fused_computation.8 | loop fusion | flops 268369920 | bytes 268960768 | tf_op jit(solution)/shard_map/reduce_sum | solution.py:60
  552.4 1.5 reshape_multiply_fusion.1
  553.9 0.1 copy.165
  554.1 101.8 %fusion.82 = f32[8,4,2048,128]{2,3,1,0:T(8,128)} fusion(bf16[1024,8,128,1]{0,2,3,1:T(8,128)(2,1)S(1)} %bitcast.361, f32[8,1024,2048,4]{2,1,3,0:T(8,128)} %get-tuple-element.22, f32[8,4,2048]{2,1,0:T(4,128)S(1)} %get-tuple-element.21, pred[1024]{0:T(1024)(128)(4,1)S(1)} %add_compare_fusion, f32[8,4,2048]{2,1,0:T(4,128)S(1)} %bitcast.345), kind=kOutput, calls=%fused_computation.86 | convolution fusion | flops 17456693248 | bytes 304612352 | tf_op jit(solution)/shard_map/kgts,skd->kgtd/dot_general | solution.py:61
  655.9 23.6 %pad_maximum_fusion = f32[8,4,2048,129]{2,3,1,0:T(8,128)} fusion(f32[8,4,2048,1]{2,3,1,0:T(1,128)S(1)} %get-tuple-element.7, f32[8,4,2048,128]{2,3,1,0:T(8,128)} %fusion.82), kind=kLoop, calls=%fused_computation.44 | loop fusion | flops 8454144 | bytes 67633152 | tf_op jit(solution)/shard_map/concatenate | solution.py:63
  679.6 0.6 copy-done.7
  680.2 0.6 slice_convert_fusion
  680.8 44.6 %fusion.316 = (bf16[1,32,128,4096]{3,2,1,0:T(8,128)(2,1)}, bf16[1,32,128,4096]{3,2,1,0:T(8,128)(2,1)}) fusion(bf16[2,32,128,4096]{3,2,1,0:T(8,128)(2,1)} %param.30), kind=kLoop, calls=%fused_computation.247 | loop fusion | bytes 134217728 | tf_op jit(solution)/shard_map/slice | solution.py:66
  725.4 160.3 %reduce-scatter.3.cloned.1.call-done = f32[8,4,256,129]{2,3,1,0:T(8,128)} async-done(((f32[8,4,2048,129]{2,3,1,0:T(8,128)}), f32[8,4,256,129]{2,3,1,0:T(8,128)}) %reduce-scatter.3.cloned.1.call-update) | async-done | bytes 4227088 | tf_op jit(solution)/shard_map/reduce_scatter | solution.py:64
  885.7 1.0 slice.129
  886.7 17.8 fusion.216
  904.5 48.4 %fusion.22 = f32[256,14336]{1,0:T(8,128)} fusion(bf16[2,4096,14336]{2,1,0:T(8,128)(2,1)} %param.31, bf16[256,4096]{1,0:T(8,128)(2,1)} %get-tuple-element.24, f32[4096]{0:T(1024)S(1)} %bitcast.358, f32[256]{0:T(256)S(1)} %add_rsqrt_fusion.3), kind=kOutput, calls=%fused_computation.26 | convolution fusion | flops 30068965376 | bytes 134235136 | tf_op jit(solution)/shard_map/dot_general | solution.py:70
  952.8 47.8 %fusion.93.clone.5.clone.5 = bf16[256,14336]{1,0:T(8,128)(2,1)} fusion(bf16[2,4096,14336]{2,1,0:T(8,128)(2,1)} %param.32, f32[256,14336]{1,0:T(8,128)} %fusion.22, bf16[256,4096]{1,0:T(8,128)(2,1)S(1)} %copy-done.17, f32[4096]{0:T(1024)S(1)} %bitcast.359, f32[256]{0:T(256)S(1)} %add_rsqrt_fusion.3), kind=kOutput, calls=%fused_computation.89.clone.clone.clone.clone.clone.clone.clone.clone.clone.2 | convolution fusion | flops 30090985472 | bytes 141575168 | tf_op jit(solution)/shard_map/dot_general | solution.py:71
  1000.7 44.1 %fusion.219 = (f32[256]{0:T(256)S(1)}, bf16[256,4096]{1,0:T(8,128)(2,1)S(1)}) fusion(bf16[2,14336,4096]{2,1,0:T(8,128)(2,1)} %param.33, bf16[256,4096]{1,0:T(8,128)(2,1)} %get-tuple-element.24, bf16[256,14336]{1,0:T(8,128)(2,1)} %fusion.93.clone.5.clone.5), kind=kOutput, calls=%fused_computation.173 | convolution fusion | flops 30071062528 | bytes 128975872 | tf_op jit(solution)/shard_map/dot_general | solution.py:73
  1044.8 16.9 fusion.191
  1061.8 16.2 fusion.194
  1078.0 15.9 fusion.290
  1094.0 52.0 %all-gather.13.cloned.1.call-done = bf16[2048,4096]{1,0:T(8,128)(2,1)} async-done(((bf16[256,4096]{1,0:T(8,128)(2,1)}), bf16[2048,4096]{1,0:T(8,128)(2,1)}) %all-gather.13.cloned.1.call-update) | async-done | bytes 16777232 | tf_op jit(solution)/shard_map/all_gather | solution.py:43
  1146.0 29.9 %fusion.31 = (f32[32,256]{1,0:T(8,128)S(1)}, f32[32,256,2048]{2,1,0:T(8,128)}) fusion(pred[256,2048]{1,0:T(8,128)(4,1)S(1)} %copy-done.1, bf16[32,32,8,128]{3,2,1,0:T(8,128)(2,1)S(1)} %fusion.290, bf16[2048,4096]{1,0:T(8,128)(2,1)} %all-gather.13.cloned.1.call-done), kind=kOutput, calls=%fused_computation.39 | convolution fusion | flops 4345290752 | bytes 86540288 | tf_op jit(solution)/shard_map/thd,shd->hts/dot_general | solution.py:45
  1175.9 21.5 %fusion.34 = f32[32,256]{1,0:T(8,128)S(1)} fusion(f32[32,256,2048]{2,1,0:T(8,128)} %get-tuple-element.28, f32[32,256]{1,0:T(8,128)S(1)} %get-tuple-element.27, pred[256,2048]{1,0:T(8,128)(4,1)S(1)} %copy-done.1), kind=kLoop, calls=%fused_computation.42 | loop fusion | flops 67100672 | bytes 67698688 | tf_op jit(solution)/shard_map/reduce_sum | solution.py:49
  1197.4 34.5 %all-gather.15.cloned.1.call-done = bf16[2048,4096]{1,0:T(8,128)(2,1)} async-done(((bf16[256,4096]{1,0:T(8,128)(2,1)}), bf16[2048,4096]{1,0:T(8,128)(2,1)}) %all-gather.15.cloned.1.call-update) | async-done | bytes 16777232 | tf_op jit(solution)/shard_map/all_gather | solution.py:44
  1231.9 31.6 %divide_convert_fusion.3.clone.5 = bf16[32,256,128]{2,1,0:T(8,128)(2,1)} fusion(f32[32,256,2048]{2,1,0:T(8,128)} %get-tuple-element.28, f32[32,256]{1,0:T(8,128)S(1)} %get-tuple-element.27, pred[256,2048]{1,0:T(8,128)(4,1)S(1)} %copy-done.1, f32[32,256]{1,0:T(8,128)S(1)} %fusion.34, ...), kind=kOutput, calls=%fused_computation.186.clone.clone.clone.clone.2 | convolution fusion | flops 4364173312 | bytes 86573056 | tf_op jit(solution)/shard_map/hts,shd->htd/dot_general | solution.py:48
  1263.5 15.3 fusion.222
  1278.8 16.9 fusion.197
  1295.8 13.9 fusion.284
  1309.7 14.8 fusion.287
  1324.5 55.4 %all-gather.17.cloned.1.call-done = bf16[2048,4096]{1,0:T(8,128)(2,1)} async-done(((bf16[256,4096]{1,0:T(8,128)(2,1)}), bf16[2048,4096]{1,0:T(8,128)(2,1)}) %all-gather.17.cloned.1.call-update) | async-done | bytes 16777232 | tf_op jit(solution)/shard_map/all_gather | solution.py:53
  1379.9 27.4 %reshape.104 = bf16[2048,8,4,128]{3,2,1,0:T(4,128)(2,1)} reshape(bf16[2048,4096]{1,0:T(8,128)(2,1)} %all-gather.17.cloned.1.call-done) | data formatting | bytes 33554432 | tf_op jit(solution)/shard_map/reshape | solution.py:53
  1407.3 94.5 %bitcast_reduce_fusion = (f32[8,4,2048]{2,1,0:T(4,128)S(1)}, f32[8,1024,2048,4]{2,1,3,0:T(8,128)}) fusion(pred[1024]{0:T(1024)(128)(4,1)S(1)} %copy-done.3, bf16[1024,8,128,1]{0,2,3,1:T(8,128)(2,1)S(1)} %bitcast.343, bf16[2048,8,4,128]{3,2,1,0:T(4,128)(2,1)} %reshape.104), kind=kOutput, calls=%fused_computation.1 | convolution fusion | flops 17381130240 | bytes 287572992 | tf_op jit(solution)/shard_map/tkgd,skd->kgts/dot_general | solution.py:56
  1501.8 0.9 broadcast_in_dim.56
  1502.7 0.0 reduce-scatter.5.cloned.1.call-start
  1502.8 81.1 %fusion.4 = f32[8,4,2048]{2,1,0:T(4,128)S(1)} fusion(f32[8,1024,2048,4]{2,1,3,0:T(8,128)} %get-tuple-element.32, f32[8,4,2048]{2,1,0:T(4,128)S(1)} %get-tuple-element.31, pred[1024]{0:T(1024)(128)(4,1)S(1)} %copy-done.3), kind=kLoop, calls=%fused_computation.10 | loop fusion | flops 268369920 | bytes 268960768 | tf_op jit(solution)/shard_map/reduce_sum | solution.py:60
  1583.9 1.5 reshape_multiply_fusion
  1585.5 0.1 copy.164
  1585.6 101.8 %fusion.85 = f32[8,4,2048,128]{2,3,1,0:T(8,128)} fusion(bf16[1024,8,128,1]{0,2,3,1:T(8,128)(2,1)S(1)} %bitcast.360, f32[8,1024,2048,4]{2,1,3,0:T(8,128)} %get-tuple-element.32, f32[8,4,2048]{2,1,0:T(4,128)S(1)} %get-tuple-element.31, pred[1024]{0:T(1024)(128)(4,1)S(1)} %copy-done.3, f32[8,4,2048]{2,1,0:T(4,128)S(1)} %bitcast.344), kind=kOutput, calls=%fused_computation.87 | convolution fusion | flops 17456693248 | bytes 304612352 | tf_op jit(solution)/shard_map/kgts,skd->kgtd/dot_general | solution.py:61
  1687.4 23.6 %pad_maximum_fusion.1 = f32[8,4,2048,129]{2,3,1,0:T(8,128)} fusion(f32[8,4,2048,1]{2,3,1,0:T(1,128)S(1)} %get-tuple-element.5, f32[8,4,2048,128]{2,3,1,0:T(8,128)} %fusion.85), kind=kLoop, calls=%fused_computation.45 | loop fusion | flops 8454144 | bytes 67633152 | tf_op jit(solution)/shard_map/concatenate | solution.py:63
  1711.0 206.2 %reduce-scatter.5.cloned.1.call-done = f32[8,4,256,129]{2,3,1,0:T(8,128)} async-done(((f32[8,4,2048,129]{2,3,1,0:T(8,128)}), f32[8,4,256,129]{2,3,1,0:T(8,128)}) %reduce-scatter.5.cloned.1.call-update) | async-done | bytes 4227088 | tf_op jit(solution)/shard_map/reduce_scatter | solution.py:64
  1917.2 1.0 slice.131
  1918.2 17.8 fusion.225
  1936.0 53.5 %fusion.16 = f32[256,14336]{1,0:T(8,128)} fusion(bf16[2,4096,14336]{2,1,0:T(8,128)(2,1)} %param.31, bf16[256,4096]{1,0:T(8,128)(2,1)} %get-tuple-element.34, f32[4096]{0:T(1024)S(1)} %bitcast.352, f32[256]{0:T(256)S(1)} %add_rsqrt_fusion), kind=kOutput, calls=%fused_computation.20 | convolution fusion | flops 30068965376 | bytes 134235136 | tf_op jit(solution)/shard_map/dot_general | solution.py:70
  1989.6 47.4 %fusion.88.clone.9 = bf16[256,14336]{1,0:T(8,128)(2,1)} fusion(bf16[2,4096,14336]{2,1,0:T(8,128)(2,1)} %param.32, f32[256,14336]{1,0:T(8,128)} %fusion.16, bf16[256,4096]{1,0:T(8,128)(2,1)S(1)} %copy-done.18, f32[4096]{0:T(1024)S(1)} %bitcast.353, f32[256]{0:T(256)S(1)} %add_rsqrt_fusion), kind=kOutput, calls=%fused_computation.88.clone.clone.clone.clone.clone.clone.clone.2 | convolution fusion | flops 30090985472 | bytes 141575168 | tf_op jit(solution)/shard_map/dot_general | solution.py:71
  2036.9 44.6 %fusion.205 = bf16[256,4096]{1,0:T(8,128)(2,1)} fusion(bf16[2,14336,4096]{2,1,0:T(8,128)(2,1)} %param.33, bf16[256,4096]{1,0:T(8,128)(2,1)S(1)} %copy-done.18, bf16[256,14336]{1,0:T(8,128)(2,1)} %fusion.88.clone.9), kind=kOutput, calls=%fused_computation.163 | convolution fusion | flops 30067916800 | bytes 128974848 | tf_op jit(solution)/shard_map/dot_general | solution.py:73
  (66 shorter events, 0.6 us)
Async XLA Ops:
  6.5 107.4 %all-gather.7.cloned.1.call-start = ((), (), s32[]{:S(2)}) async-start(), calls=%async_computation.2 | async-start | bytes 18874368 | tf_op jit(solution)/shard_map/all_gather | solution.py:43
  10.0 16.9 copy-start.4
  26.9 17.0 copy-start.6
  26.9 173.0 %all-gather.9.cloned.1.call-start = ((), (), s32[]{:S(2)}) async-start(), calls=%async_computation.3 | async-start | bytes 18874368 | tf_op jit(solution)/shard_map/all_gather | solution.py:44
  43.1 305.3 %all-gather.11.cloned.1.call-start = ((), (), s32[]{:S(2)}) async-start(), calls=%async_computation.4 | async-start | bytes 18874368 | tf_op jit(solution)/shard_map/all_gather | solution.py:53
  43.9 156.0 %copy-start = (pred[256,2048]{1,0:T(8,128)(4,1)}, pred[256,2048]{1,0:T(8,128)(4,1)S(1)}, u32[]{:S(2)}) copy-start(pred[256,2048]{1,0:T(8,128)(4,1)S(1)} %iota_compare_fusion) | copy-start | bytes 1572868
  165.4 66.2 %copy-start.5 = (bf16[256,4096]{1,0:T(8,128)(2,1)S(1)}, bf16[256,4096]{1,0:T(8,128)(2,1)}, u32[]{:S(2)}) copy-start(bf16[256,4096]{1,0:T(8,128)(2,1)} %param.17) | copy-start | bytes 6291460
  264.3 288.2 %all-reduce.3.cloned.1.call-start = ((), (), s32[]{:S(2)}) async-start(), calls=%async_computation.5 | async-start | bytes 524288 | tf_op jit(solution)/shard_map/pmax | solution.py:62
  265.0 289.1 %copy-start.2 = (pred[1024]{0:T(1024)(128)(4,1)}, pred[1024]{0:T(1024)(128)(4,1)S(1)}, u32[]{:S(2)}) copy-start(pred[1024]{0:T(1024)(128)(4,1)S(1)} %add_compare_fusion) | copy-start | bytes 3076
  471.4 414.3 %reduce-scatter.3.cloned.1.call-start = ((), (), s32[]{:S(2)}) async-start(), calls=%async_computation.6 | async-start | bytes 40108032 | tf_op jit(solution)/shard_map/reduce_scatter | solution.py:64
  471.5 82.6 %copy-start.12 = (bf16[1024,1024]{0,1:T(8,128)(2,1)S(1)}, bf16[1024,1024]{0,1:T(8,128)(2,1)}, u32[]{:S(2)}) copy-start(bf16[1024,1024]{0,1:T(8,128)(2,1)} %fusion.281) | copy-start | bytes 6291460
  679.5 0.7 copy-start.7
  679.5 466.4 %all-gather.13.cloned.1.call-start = ((), (), s32[]{:S(2)}) async-start(), calls=%async_computation.7 | async-start | bytes 18874368 | tf_op jit(solution)/shard_map/all_gather | solution.py:43
  680.8 205.9 %copy-start.13 = (bf16[256,4096]{1,0:T(8,128)(2,1)S(1)}, bf16[256,4096]{1,0:T(8,128)(2,1)}, u32[]{:S(2)}) copy-start(bf16[256,4096]{1,0:T(8,128)(2,1)} %get-tuple-element.20) | copy-start | bytes 6291460
  904.5 48.4 %copy-start.17 = (bf16[256,4096]{1,0:T(8,128)(2,1)S(1)}, bf16[256,4096]{1,0:T(8,128)(2,1)}, u32[]{:S(2)}) copy-start(bf16[256,4096]{1,0:T(8,128)(2,1)} %get-tuple-element.24) | copy-start | bytes 6291460
  1000.6 44.2 %copy-start.8 = (f32[1,4096]{1,0:T(1,128)S(1)}, f32[1,4096]{1,0:T(1,128)}, u32[]{:S(2)}) copy-start(f32[1,4096]{1,0:T(1,128)} %get-tuple-element.15) | copy-start | bytes 49156
  1044.8 17.0 copy-start.16
  1061.7 170.1 %all-gather.15.cloned.1.call-start = ((), (), s32[]{:S(2)}) async-start(), calls=%async_computation.8 | async-start | bytes 18874368 | tf_op jit(solution)/shard_map/all_gather | solution.py:44
  1078.0 68.0 %copy-start.1 = (pred[256,2048]{1,0:T(8,128)(4,1)S(1)}, pred[256,2048]{1,0:T(8,128)(4,1)}, u32[]{:S(2)}) copy-start(pred[256,2048]{1,0:T(8,128)(4,1)} %copy-done) | copy-start | bytes 1572868
  1078.0 301.9 %all-gather.17.cloned.1.call-start = ((), (), s32[]{:S(2)}) async-start(), calls=%async_computation.9 | async-start | bytes 18874368 | tf_op jit(solution)/shard_map/all_gather | solution.py:53
  1263.5 15.3 copy-start.9
  1278.8 16.9 copy-start.14
  1295.7 288.2 %all-reduce.5.cloned.1.call-start = ((), (), s32[]{:S(2)}) async-start(), calls=%async_computation.10 | async-start | bytes 524288 | tf_op jit(solution)/shard_map/pmax | solution.py:62
  1324.5 82.8 %copy-start.3 = (pred[1024]{0:T(1024)(128)(4,1)S(1)}, pred[1024]{0:T(1024)(128)(4,1)}, u32[]{:S(2)}) copy-start(pred[1024]{0:T(1024)(128)(4,1)} %copy-done.2) | copy-start | bytes 3076
  1502.7 414.5 %reduce-scatter.5.cloned.1.call-start = ((), (), s32[]{:S(2)}) async-start(), calls=%async_computation.11 | async-start | bytes 40108032 | tf_op jit(solution)/shard_map/reduce_scatter | solution.py:64
  1502.8 82.8 %copy-start.11 = (bf16[1024,1024]{0,1:T(8,128)(2,1)S(1)}, bf16[1024,1024]{0,1:T(8,128)(2,1)}, u32[]{:S(2)}) copy-start(bf16[1024,1024]{0,1:T(8,128)(2,1)} %fusion.287) | copy-start | bytes 6291460
  1711.0 207.2 %copy-start.15 = (bf16[256,4096]{1,0:T(8,128)(2,1)S(1)}, bf16[256,4096]{1,0:T(8,128)(2,1)}, u32[]{:S(2)}) copy-start(bf16[256,4096]{1,0:T(8,128)(2,1)} %copy-done.14) | copy-start | bytes 6291460
  1918.2 17.8 copy-start.10
  1936.0 53.6 %copy-start.18 = (bf16[256,4096]{1,0:T(8,128)(2,1)S(1)}, bf16[256,4096]{1,0:T(8,128)(2,1)}, u32[]{:S(2)}) copy-start(bf16[256,4096]{1,0:T(8,128)(2,1)} %get-tuple-element.34) | copy-start | bytes 6291460
Sparse Core Ops, SparseCore 0:
  27.0 86.9 all-gather.6
  115.8 84.0 all-gather.8
  264.4 84.0 all-gather.10
  471.5 42.6 all-reduce.2
  679.6 206.0 reduce-scatter.2
  1061.9 84.0 all-gather.12
  1147.8 84.0 all-gather.14
  1295.8 84.0 all-gather.16
  1502.8 42.6 all-reduce.4
  1711.1 206.0 reduce-scatter.4
where the time goes:
time: 2100 us; the launch traced here: 2090 us
  matrix products  1060 us (50%)
  waiting for transfers between devices  652 us (31%)
  other arithmetic  260 us (12%)
  local copies, waits for them, and re-layouts  104 us (5%)
    reduce_scatter x2, waiting for transfers between devices, local_step(): combined = lax.psum_scatter(packed, 'sp', scatter_dimension=2, tiled=True)  367 us
    dot_general x2, matrix products, local_step(): jnp.einsum('kgts,skd->kgtd', weights.astype(jnp.bfloat16), mem_values, pr...  204 us
    dot_general x2, matrix products, local_step(): jnp.einsum('tkgd,skd->kgts', cross_queries, mem_keys, preferred_element_t...  189 us
    dot_general x12, matrix products, project(): jnp.dot(acts, weight_mat, preferred_element_type=jnp.float32)  189 us
    reduce_sum x2, other arithmetic, local_step(): part_sum = jnp.sum(weights, axis=-1, keepdims=True)  162 us
    all_gather x2, waiting for transfers between devices, local_step(): lax.all_gather(project(normed, cross_q[layer]), 'sp', axis=0, tiled=True)  110 us
    all_gather x2, waiting for transfers between devices, local_step(): lax.all_gather(project(normed, self_k[layer]), 'sp', axis=0, tiled=True)  106 us
    dot_general x2, matrix products, local_step(): jnp.dot(normed, mlp_gate[layer], preferred_element_type=jnp.float32)  102 us
  transfers between devices with their start and end apart: 10, of which 8 were waited for; matrix products, arithmetic and copies ran while one was open for 21% of the time, Pallas kernels for 0%

commit v1 on v0

v1 whole, which is shorter than its diff:
```python
import functools

import jax
import jax.numpy as jnp
from jax import lax
from jax.experimental import pallas as pl
from jax.experimental.pallas import tpu as pltpu
from jax.sharding import PartitionSpec as P

EPS = 1e-6
NEG_BIG = -1e30
LOG2E = 1.4426950408889634
MESH = pl.DeviceIdType.MESH
VMEM_LIMIT = 66_000_000
BF16 = jnp.bfloat16
F32 = jnp.float32


def norm_rows(hidden, gain):
    h = hidden.astype(F32)
    inv = lax.rsqrt(jnp.mean(h * h, axis=-1, keepdims=True) + EPS)
    return (h * inv * gain.astype(F32)).astype(BF16)


def dot(a, b):
    return jnp.dot(a, b, preferred_element_type=F32)


def dot_t(a, b):
    return lax.dot_general(a, b, (((1,), (1,)), ((), ())), preferred_element_type=F32)


def params(collective_id, dims=1):
    return pltpu.CompilerParams(
        collective_id=collective_id,
        has_side_effects=collective_id is not None,
        vmem_limit_bytes=VMEM_LIMIT,
        dimension_semantics=("arbitrary",) * dims,
    )


class Exchange:
    def __init__(self, group):
        self.group = group
        self.me = lax.axis_index("sp")
        self.dp = lax.axis_index("dp")

    def peer(self, offset):
        return lax.rem(self.me + offset, self.group)

    def greet(self):
        barrier = pltpu.get_barrier_semaphore()
        for k in range(1, self.group):
            pl.semaphore_signal(
                barrier, inc=1, device_id=(self.dp, self.peer(k)), device_id_type=MESH
            )

    def await_all(self):
        pl.semaphore_wait(pltpu.get_barrier_semaphore(), self.group - 1)

    def copy(self, src, dst, send, recv, target):
        return pltpu.make_async_remote_copy(
            src_ref=src, dst_ref=dst, send_sem=send, recv_sem=recv,
            device_id=(self.dp, target), device_id_type=MESH,
        )


def qkv_kernel(group, layer, mem_layers, refs):
    n_w = 3
    it = iter(refs)
    hid, gain = next(it), next(it)
    w = [next(it) for _ in range(n_w)]
    if mem_layers:
        mem, ck, cv = next(it), next(it), next(it)
    out = next(it)
    if mem_layers:
        kv_out, kv_keep = next(it), next(it)
    x, buf, ssem, rsem, lsem = (next(it) for _ in range(5))
    if mem_layers:
        mem_v, kv_buf, kv_buf1, kvs, kvr, kvl, keep_sem, mem_sem = (next(it) for _ in range(8))
    ex = Exchange(group)
    me = ex.me
    i = pl.program_id(0)
    rows = hid.shape[0]
    width = buf.shape[2]
    half = width // 2
    n_steps = n_w * group * 2

    @pl.when(i == 0)
    def _():
        ex.greet()
        if mem_layers:
            pltpu.make_async_copy(mem, mem_v, mem_sem).start()
        x[...] = norm_rows(hid[...], gain[layer : layer + 1, :])

    @pl.when(i == 1)
    def _():
        ex.await_all()

    for t in range(n_w):

        @pl.when((i >= t * group * 2) & (i < (t + 1) * group * 2))
        def _(t=t):
            slot = lax.div(i, 2)
            res = dot(x[...], w[t][0]).astype(BF16)

            @pl.when(lax.rem(i, 2) == 0)
            def _():
                buf[slot, :, 0:half] = res

            @pl.when(lax.rem(i, 2) == 1)
            def _():
                buf[slot, :, half:width] = res

    def out_at(t, p):
        return out.at[t, pl.ds(pl.multiple_of(p * rows, rows), rows)]

    def block_copy(slot):
        t, r = lax.div(slot, group), lax.rem(slot, group)
        return t, r, ex.copy(
            buf.at[slot], out_at(t, me), ssem.at[slot], rsem.at[t, me], ex.peer(r + 1)
        )

    def own_copy(t):
        return pltpu.make_async_copy(buf.at[t * group + group - 1], out_at(t, me), lsem.at[t])

    @pl.when((i >= 2) & (i <= n_steps) & (lax.rem(i, 2) == 0))
    def _():
        slot = lax.div(i, 2) - 1
        t, r, cp = block_copy(slot)

        @pl.when(r < group - 1)
        def _():
            cp.start()

        @pl.when(r == group - 1)
        def _():
            own_copy(t).start()

    last = n_steps
    if mem_layers:
        pairs = group // 2
        hd = ck.shape[2] // 2
        mem_rows = mem.shape[0]
        senders = kv_out.shape[0]
        base = n_steps
        last = n_steps + mem_layers * pairs * 2

        @pl.when(i == base)
        def _():
            pltpu.make_async_copy(mem, mem_v, mem_sem).wait()

        bufs = (kv_buf, kv_buf1)
        for m in range(mem_layers):
            b0 = base + m * pairs * 2

            @pl.when((i >= b0) & (i < b0 + pairs * 2))
            def _(m=m, b0=b0):
                j = i - b0
                pair = lax.div(j, 2)
                for kind, wref in enumerate((ck, cv)):

                    @pl.when((lax.rem(j, 2) == kind) & (me < senders))
                    def _(kind=kind, wref=wref):
                        for c in range(4):
                            q4 = mem_rows // 4
                            rs = slice(c * q4, (c + 1) * q4)
                            res = dot(mem_v[rs, :], wref[0]).astype(BF16)
                            for side in range(2):
                                bufs[m][2 * pair + side, rs, kind * hd : (kind + 1) * hd] = res[
                                    :, side * hd : (side + 1) * hd
                                ]

        def kv_copy(d):
            return ex.copy(kv_buf.at[d], kv_out.at[me], kvs.at[d], kvr.at[me], d)

        @pl.when((i > base) & (i <= base + pairs * 2) & (lax.rem(i - base, 2) == 0) & (me < senders))
        def _():
            pair = lax.div(i - base, 2) - 1
            for side in range(2):
                d = 2 * pair + side

                @pl.when(d != me)
                def _():
                    kv_copy(d).start()

                @pl.when(d == me)
                def _():
                    pltpu.make_async_copy(kv_buf.at[d], kv_out.at[me], kvl).start()

        keep_copy = pltpu.make_async_copy(kv_buf1, kv_keep, keep_sem)

        @pl.when(i == last)
        def _():
            keep_copy.start()

    @pl.when(i == last)
    def _():
        for t in range(n_w):
            own_copy(t).wait()
            for k in range(1, group):
                p = ex.peer(k)
                ex.copy(buf.at[0], out_at(t, p), ssem.at[t * group + k - 1], rsem.at[t, p], p).wait()
        if mem_layers:

            @pl.when(me < senders)
            def _():
                pltpu.make_async_copy(kv_buf.at[0], kv_out.at[me], kvl).wait()
                for k in range(1, group):
                    kv_copy(ex.peer(k)).wait_send()

            for p in range(senders):

                @pl.when(me != p)
                def _(p=p):
                    ex.copy(kv_buf.at[0], kv_out.at[p], kvs.at[0], kvr.at[p], p).wait_recv()

            keep_copy.wait()


def qkv_call(mesh, layer, hidden, gain, ws, mem=None, ck=None, cv=None):
    group = mesh.shape["sp"]
    rows, width = hidden.shape
    per_dev = ws[0].shape[2] // group
    tn = per_dev // 2
    n_steps = 3 * group * 2
    mem_layers = 0 if mem is None else ck.shape[0]

    def w_map(t):
        def index(i):
            j = jnp.clip(i - t * group * 2, 0, group * 2 - 1)
            d = lax.rem(lax.axis_index("sp") + 1 + lax.div(j, 2), group)
            return layer, 0, d * 2 + lax.rem(j, 2)

        return index

    in_specs = [
        pl.BlockSpec((rows, width), lambda i: (0, 0), pipeline_mode=pl.Buffered(1)),
        pl.BlockSpec(gain.shape, lambda i: (0, 0), pipeline_mode=pl.Buffered(1)),
    ] + [pl.BlockSpec((1, width, tn), w_map(t)) for t in range(3)]
    args = [hidden, gain, *ws]
    out_shape = [jax.ShapeDtypeStruct((3, rows * group, per_dev), BF16)]
    scratch = [
        pltpu.VMEM((rows, width), BF16),
        pltpu.VMEM((3 * group, rows, per_dev), BF16),
        pltpu.SemaphoreType.DMA((3 * group,)),
        pltpu.SemaphoreType.DMA((3, group)),
        pltpu.SemaphoreType.DMA((3,)),
    ]
    last = n_steps
    if mem_layers:
        mem_rows = mem.shape[0]
        hd = ck.shape[2] // group
        pairs = group // 2
        senders = group * 3 // 4

        def kv_map(i):
            j = jnp.clip(i - n_steps, 0, mem_layers * pairs * 2 - 1)
            return lax.div(j, pairs * 2), 0, lax.div(lax.rem(j, pairs * 2), 2)

        in_specs += [
            pl.BlockSpec(memory_space=pl.ANY),
            pl.BlockSpec((1, width, 2 * hd), kv_map),
            pl.BlockSpec((1, width, 2 * hd), kv_map),
        ]
        args += [mem, ck, cv]
        out_shape += [
            jax.ShapeDtypeStruct((senders, mem_rows, 2 * hd), BF16),
            jax.ShapeDtypeStruct((group, mem_rows, 2 * hd), BF16),
        ]
        scratch += [
            pltpu.VMEM((mem_rows, width), BF16),
            pltpu.VMEM((group, mem_rows, 2 * hd), BF16),
            pltpu.VMEM((group, mem_rows, 2 * hd), BF16),
            pltpu.SemaphoreType.DMA((group,)),
            pltpu.SemaphoreType.DMA((group,)),
            pltpu.SemaphoreType.DMA,
            pltpu.SemaphoreType.DMA,
            pltpu.SemaphoreType.DMA,
        ]
        last = n_steps + mem_layers * pairs * 2

    def body(*refs):
        qkv_kernel(group, layer, mem_layers, refs)

    return pl.pallas_call(
        body,
        grid=(last + 1,),
        in_specs=in_specs,
        out_specs=[pl.BlockSpec(memory_space=pl.ANY)] * len(out_shape),
        out_shape=out_shape,
        scratch_shapes=scratch,
        compiler_params=params(layer),
        name=f"qkv{layer}",
    )(*args)


def send_back(ex, i, group, rows, cols, buf, out, ssem, rsem, lsem):
    me = ex.me

    def out_at(p):
        return out.at[:, pl.ds(pl.multiple_of(p * cols, cols), cols)]

    own = pltpu.make_async_copy(buf.at[group - 1], out_at(me), lsem)

    @pl.when((i >= 1) & (i < group))
    def _():
        r = i - 1
        ex.copy(buf.at[r], out_at(me), ssem.at[r], rsem.at[me], ex.peer(r + 1)).start()

    @pl.when(i == group)
    def _():
        own.start()
        for k in range(1, group):
            p = ex.peer(k)
            ex.copy(buf.at[k - 1], out_at(p), ssem.at[k - 1], rsem.at[p], p).wait()
        own.wait()


def self_kernel(group, hd, qkv, out, buf, ssem, rsem, lsem, m_s, l_s, acc_s):
    ex = Exchange(group)
    i = pl.program_id(0)
    rows, cols = buf.shape[1], buf.shape[2]
    heads = cols // hd
    bk = 2 * rows
    coef = hd**-0.5 * LOG2E

    @pl.when(i == 0)
    def _():
        ex.greet()

    @pl.when(i == 1)
    def _():
        ex.await_all()

    @pl.when(i < group)
    def _():
        d = ex.peer(i + 1)
        r0 = pl.multiple_of(d * rows, rows)
        for h in range(heads):
            m_s[h] = jnp.full((rows, 1), NEG_BIG, F32)
            l_s[h] = jnp.zeros((rows, 1), F32)
            acc_s[h] = jnp.zeros((rows, hd), F32)

        def step(kb, masked):
            k0 = pl.multiple_of(kb * bk, bk)
            if masked:
                row = r0 + lax.broadcasted_iota(jnp.int32, (rows, bk), 0)
                col = k0 + lax.broadcasted_iota(jnp.int32, (rows, bk), 1)
                allowed = row >= col
            for h in range(heads):
                hs = slice(h * hd, (h + 1) * hd)
                s = dot_t(qkv[0, pl.ds(r0, rows), hs], qkv[1, pl.ds(k0, bk), hs])
                if masked:
                    s = jnp.where(allowed, s, NEG_BIG)
                m_old = m_s[h]
                m_new = jnp.maximum(m_old, jnp.max(s, axis=-1, keepdims=True))
                p = jnp.exp2((s - m_new) * coef)
                alpha = jnp.exp2((m_old - m_new) * coef)
                l_s[h] = l_s[h] * alpha + jnp.sum(p, axis=-1, keepdims=True)
                acc_s[h] = acc_s[h] * alpha + dot(p.astype(BF16), qkv[2, pl.ds(k0, bk), hs])
                m_s[h] = m_new

        full = lax.div(d, 2)

        def loop(kb, c):
            step(kb, False)
            return c

        lax.fori_loop(0, full, loop, 0)
        step(full, True)
        for h in range(heads):
            buf[i, :, h * hd : (h + 1) * hd] = (acc_s[h] / l_s[h]).astype(BF16)

    send_back(ex, i, group, rows, cols, buf, out, ssem, rsem, lsem)


def back_scratch(group, rows, cols):
    return [
        pltpu.VMEM((group, rows, cols), BF16),
        pltpu.SemaphoreType.DMA((group,)),
        pltpu.SemaphoreType.DMA((group,)),
        pltpu.SemaphoreType.DMA,
    ]


def self_call(mesh, hd, qkv, cid):
    group = mesh.shape["sp"]
    _, all_rows, cols = qkv.shape
    rows = all_rows // group
    heads = cols // hd
    return pl.pallas_call(
        functools.partial(self_kernel, group, hd),
        grid=(group + 1,),
        in_specs=[pl.BlockSpec(qkv.shape, lambda i: (0, 0, 0), pipeline_mode=pl.Buffered(1))],
        out_specs=pl.BlockSpec(memory_space=pl.ANY),
        out_shape=jax.ShapeDtypeStruct((rows, cols * group), BF16),
        scratch_shapes=back_scratch(group, rows, cols)
        + [
            pltpu.VMEM((heads, rows, 1), F32),
            pltpu.VMEM((heads, rows, 1), F32),
            pltpu.VMEM((heads, rows, hd), F32),
        ],
        compiler_params=params(cid),
        name="self_attn",
    )(qkv)


def cross_kernel(group, hd, bk, mem_len, q, kv, out, buf, ssem, rsem, lsem, m_s, l_s, acc_s):
    ex = Exchange(group)
    i = pl.program_id(0)
    rows, cols = buf.shape[1], buf.shape[2]
    heads = cols // hd
    coef = hd**-0.5 * LOG2E
    n_kb = kv.shape[0] // bk

    @pl.when(i == 0)
    def _():
        ex.greet()

    @pl.when(i == 1)
    def _():
        ex.await_all()

    @pl.when(i < group)
    def _():
        d = ex.peer(i + 1)
        r0 = pl.multiple_of(d * rows, rows)
        for h in range(heads):
            m_s[h] = jnp.full((rows, 1), NEG_BIG, F32)
            l_s[h] = jnp.zeros((rows, 1), F32)
            acc_s[h] = jnp.zeros((rows, hd), F32)

        def loop(kb, c):
            k0 = pl.multiple_of(kb * bk, bk)
            col = k0 + lax.broadcasted_iota(jnp.int32, (1, bk), 1)
            allowed = col < mem_len[0]
            keys = kv[pl.ds(k0, bk), 0:hd]
            vals = kv[pl.ds(k0, bk), hd : 2 * hd]
            for h in range(heads):
                s = dot_t(q[pl.ds(r0, rows), h * hd : (h + 1) * hd], keys)
                s = jnp.where(allowed, s, NEG_BIG)
                m_old = m_s[h]
                m_new = jnp.maximum(m_old, jnp.max(s, axis=-1, keepdims=True))
                p = jnp.exp2((s - m_new) * coef)
                alpha = jnp.exp2((m_old - m_new) * coef)
                l_s[h] = l_s[h] * alpha + jnp.sum(p, axis=-1, keepdims=True)
                acc_s[h] = acc_s[h] * alpha + dot(p.astype(BF16), vals)
                m_s[h] = m_new
            return c

        lax.fori_loop(0, n_kb, loop, 0)
        for h in range(heads):
            buf[i, :, h * hd : (h + 1) * hd] = (acc_s[h] / l_s[h]).astype(BF16)

    send_back(ex, i, group, rows, cols, buf, out, ssem, rsem, lsem)


def cross_call(mesh, hd, mem_len, q, kv, cid):
    group = mesh.shape["sp"]
    all_rows, cols = q.shape
    rows = all_rows // group
    heads = cols // hd
    return pl.pallas_call(
        functools.partial(cross_kernel, group, hd, 1024),
        grid=(group + 1,),
        in_specs=[
            pl.BlockSpec(memory_space=pltpu.SMEM),
            pl.BlockSpec(q.shape, lambda i: (0, 0), pipeline_mode=pl.Buffered(1)),
            pl.BlockSpec(kv.shape, lambda i: (0, 0), pipeline_mode=pl.Buffered(1)),
        ],
        out_specs=pl.BlockSpec(memory_space=pl.ANY),
        out_shape=jax.ShapeDtypeStruct((rows, cols * group), BF16),
        scratch_shapes=back_scratch(group, rows, cols)
        + [
            pltpu.VMEM((heads, rows, 1), F32),
            pltpu.VMEM((heads, rows, 1), F32),
            pltpu.VMEM((heads, rows, hd), F32),
        ],
        compiler_params=params(cid),
        name="cross_attn",
    )(mem_len, q, kv)


def cross_q_kernel(group, layer, att, hid, gain, wo, wq, out, q_out, x, buf, ssem, rsem, lsem):
    ex = Exchange(group)
    me = ex.me
    i = pl.program_id(0)
    rows = hid.shape[0]
    tn = wo.shape[2]
    n_o = hid.shape[1] // tn

    @pl.when(i == 0)
    def _():
        ex.greet()

    for t in range(n_o):

        @pl.when(i == t)
        def _(t=t):
            cs = slice(t * tn, (t + 1) * tn)
            out[:, cs] = (hid[:, cs].astype(F32) + dot(att[...], wo[0])).astype(BF16)

    @pl.when(i == n_o)
    def _():
        ex.await_all()
        x[...] = norm_rows(out[...], gain[layer : layer + 1, :])

    def out_at(p):
        return q_out.at[pl.ds(pl.multiple_of(p * rows, rows), rows)]

    own = pltpu.make_async_copy(buf.at[group - 1], out_at(me), lsem)

    @pl.when((i >= n_o) & (i < n_o + group))
    def _():
        buf[i - n_o] = dot(x[...], wq[0]).astype(BF16)

    @pl.when((i > n_o) & (i < n_o + group))
    def _():
        r = i - n_o - 1
        ex.copy(buf.at[r], out_at(me), ssem.at[r], rsem.at[me], ex.peer(r + 1)).start()

    @pl.when(i == n_o + group)
    def _():
        own.start()
        for k in range(1, group):
            p = ex.peer(k)
            ex.copy(buf.at[k - 1], out_at(p), ssem.at[k - 1], rsem.at[p], p).wait()
        own.wait()


def cross_q_call(mesh, layer, att, hidden, gain, wo, wq, cid):
    group = mesh.shape["sp"]
    rows, width = hidden.shape
    tn = wq.shape[2] // group
    n_o = width // tn
    whole = pl.BlockSpec((rows, width), lambda i: (0, 0), pipeline_mode=pl.Buffered(1))

    def q_map(i):
        j = jnp.clip(i - n_o, 0, group - 1)
        return layer, 0, lax.rem(lax.axis_index("sp") + 1 + j, group)

    return pl.pallas_call(
        functools.partial(cross_q_kernel, group, layer),
        grid=(n_o + group + 1,),
        in_specs=[
            whole,
            whole,
            pl.BlockSpec(gain.shape, lambda i: (0, 0), pipeline_mode=pl.Buffered(1)),
            pl.BlockSpec((1, width, tn), lambda i: (layer, 0, jnp.minimum(i, n_o - 1))),
            pl.BlockSpec((1, width, tn), q_map),
        ],
        out_specs=[pl.BlockSpec((rows, width), lambda i: (0, 0)), pl.BlockSpec(memory_space=pl.ANY)],
        out_shape=[
            jax.ShapeDtypeStruct((rows, width), BF16),
            jax.ShapeDtypeStruct((rows * group, tn), BF16),
        ],
        scratch_shapes=[pltpu.VMEM((rows, width), BF16)] + back_scratch(group, rows, tn),
        compiler_params=params(cid),
        name=f"cross_q{layer}",
    )(att, hidden, gain, wo, wq)


def post_kernel(group, layer, counts, senders, refs):
    n_o, n_f, n_d = counts
    it = iter(refs)
    att, hid, gain, wo, wg, wu, wd = (next(it) for _ in range(7))
    keep = next(it) if senders else None
    out = next(it)
    kv_out = next(it) if senders else None
    y, x, act = (next(it) for _ in range(3))
    i = pl.program_id(0)
    tn = wo.shape[2]
    td = wd.shape[2]
    last = n_o + n_f + n_d - 1
    if senders:
        kvs, kvr, kvl = (next(it) for _ in range(3))
        ex = Exchange(group)
        me = ex.me

        def kv_copy(d):
            return ex.copy(keep.at[d], kv_out.at[me], kvs.at[d], kvr.at[me], d)

        own = pltpu.make_async_copy(keep.at[me], kv_out.at[me], kvl)

        @pl.when(i == 0)
        def _():
            ex.greet()

        @pl.when(i == 1)
        def _():
            ex.await_all()

        @pl.when((i == 1) & (me < senders))
        def _():
            own.start()
            for k in range(1, group):
                kv_copy(ex.peer(k)).start()

    for t in range(n_o):

        @pl.when(i == t)
        def _(t=t):
            cs = slice(t * tn, (t + 1) * tn)
            y[:, cs] = (hid[:, cs].astype(F32) + dot(att[...], wo[0])).astype(BF16)

    @pl.when(i == n_o)
    def _():
        x[...] = norm_rows(y[...], gain[layer : layer + 1, :])

    @pl.when((i >= n_o) & (i < n_o + n_f))
    def _():
        g = dot(x[...], wg[0])
        u = dot(x[...], wu[0])
        act[i - n_o] = (g * jax.nn.sigmoid(g) * u).astype(BF16)

    tf = wg.shape[2]
    for t in range(n_d):

        @pl.when(i == n_o + n_f + t)
        def _(t=t):
            cs = slice(t * td, (t + 1) * td)
            total = y[:, cs].astype(F32)
            acc = dot(act[0], wd[0, 0:tf, :])
            for c in range(1, n_f):
                acc += dot(act[c], wd[0, c * tf : (c + 1) * tf, :])
            out[:, cs] = (total + acc).astype(BF16)

    if senders:

        @pl.when(i == last)
        def _():
            @pl.when(me < senders)
            def _():
                own.wait()
                for k in range(1, group):
                    kv_copy(ex.peer(k)).wait_send()

            for p in range(senders):

                @pl.when(me != p)
                def _(p=p):
                    ex.copy(keep.at[p], kv_out.at[p], kvs.at[0], kvr.at[p], p).wait_recv()


def post_call(mesh, layer, att, hidden, gain, wo, wg, wu, wd, keep, cid):
    group = mesh.shape["sp"]
    rows, width = hidden.shape
    ff = wg.shape[2]
    tn, tf, td = 512, 512, 256
    n_o, n_f, n_d = width // tn, ff // tf, width // td
    senders = 0 if keep is None else group * 3 // 4
    whole = pl.BlockSpec((rows, width), lambda i: (0, 0), pipeline_mode=pl.Buffered(1))
    f_map = lambda i: (layer, 0, jnp.clip(i - n_o, 0, n_f - 1))
    in_specs = [
        whole,
        whole,
        pl.BlockSpec(gain.shape, lambda i: (0, 0), pipeline_mode=pl.Buffered(1)),
        pl.BlockSpec((1, width, tn), lambda i: (layer, 0, jnp.minimum(i, n_o - 1))),
        pl.BlockSpec((1, width, tf), f_map),
        pl.BlockSpec((1, width, tf), f_map),
        pl.BlockSpec((1, ff, td), lambda i: (layer, 0, jnp.clip(i - n_o - n_f, 0, n_d - 1))),
    ]
    args = [att, hidden, gain, wo, wg, wu, wd]
    out_specs = [pl.BlockSpec((rows, width), lambda i: (0, 0), pipeline_mode=pl.Buffered(1))]
    out_shape = [jax.ShapeDtypeStruct((rows, width), BF16)]
    scratch = [
        pltpu.VMEM((rows, width), BF16),
        pltpu.VMEM((rows, width), BF16),
        pltpu.VMEM((n_f, rows, tf), BF16),
    ]
    if senders:
        in_specs.append(pl.BlockSpec(memory_space=pl.ANY))
        args.append(keep)
        out_specs.append(pl.BlockSpec(memory_space=pl.ANY))
        out_shape.append(jax.ShapeDtypeStruct((senders,) + keep.shape[1:], BF16))
        scratch += [
            pltpu.SemaphoreType.DMA((group,)),
            pltpu.SemaphoreType.DMA((group,)),
            pltpu.SemaphoreType.DMA,
        ]

    def body(*refs):
        post_kernel(group, layer, (n_o, n_f, n_d), senders, refs)

    return pl.pallas_call(
        body,
        grid=(n_o + n_f + n_d,),
        in_specs=in_specs,
        out_specs=out_specs,
        out_shape=out_shape,
        scratch_shapes=scratch,
        compiler_params=params(cid if senders else None),
        name=f"post{layer}",
    )(*args)


def solution(mesh):
    row_spec = P(("dp", "sp"), None)

    def local_step(hidden, memory, mem_len, norm_self, norm_cross, norm_mlp, self_q, self_k, self_v, self_o, cross_q, cross_k, cross_v, cross_o, mlp_gate, mlp_up, mlp_down):
        layers, _, hd, width = self_o.shape
        self_o = self_o.reshape(layers, -1, width)
        cross_o = cross_o.reshape(layers, -1, width)
        keep = None
        for layer in range(layers):
            if layer == 0:
                qkv, kv, keep = qkv_call(mesh, layer, hidden, norm_self, (self_q, self_k, self_v), memory, cross_k, cross_v)
            else:
                (qkv,) = qkv_call(mesh, layer, hidden, norm_self, (self_q, self_k, self_v))
            att = self_call(mesh, hd, qkv, layers)
            hidden, q = cross_q_call(mesh, layer, att, hidden, norm_cross, self_o, cross_q, layers + 1 + layer)
            att = cross_call(mesh, hd, mem_len, q, kv.reshape(-1, 2 * hd), 2 * layers + 1)
            res = post_call(mesh, layer, att, hidden, norm_mlp, cross_o, mlp_gate, mlp_up, mlp_down, keep, 2 * layers + 2)
            hidden = res[0]
            if layer == 0:
                kv, keep = res[1], None
        return hidden

    return jax.shard_map(local_step, mesh=mesh, in_specs=(row_spec, row_spec, P("dp")) + (P(),) * 14, out_specs=row_spec, check_vma=False)
```

time: 2100 us -> 1030 us (0.49)
  matrix products: 1060 us -> 0 us
  Pallas kernels: 0 us -> 1010 us
  waiting for transfers between devices: 652 us -> 0 us
  other arithmetic: 260 us -> 0 us
  local copies, waits for them, and re-layouts: 104 us -> 0 us
    dot_general x30 -> x0, matrix products: 1060 us -> none  [the longest x2 204 us: local_step(): jnp.einsum('kgts,skd->kgtd', weights.astype(jnp.bfloat16), mem_values, pr...]
    pallas_call x0 -> x10, Pallas kernels: none -> 1010 us  [the longest x2 336 us: post_call(): pl.pallas_call(body, grid=(n_o + n_f + n_d,), in_specs=in_specs, out_spec...]
    reduce_scatter x2 -> x0, waiting for transfers between devices: 367 us -> none  [local_step(): combined = lax.psum_scatter(packed, 'sp', scatter_dimension=2, tiled=True)]
    all_gather x6 -> x0, waiting for transfers between devices: 285 us -> none  [the longest x2 110 us: local_step(): lax.all_gather(project(normed, cross_q[layer]), 'sp', axis=0, tiled=True)]
    reduce_sum x5 -> x0, other arithmetic: 207 us -> none  [the longest x2 162 us: local_step(): part_sum = jnp.sum(weights, axis=-1, keepdims=True)]
    reshape x2 -> x0, local copies, waits for them, and re-layouts: 54.8 us -> none  [local_step(): lax.all_gather(project(normed, cross_q[layer]), 'sp', axis=0, tiled=True)]
    concatenate x2 -> x0, other arithmetic: 47.1 us -> none  [local_step(): packed = jnp.concatenate([part_num * rescale, part_sum * rescale], axis=-1)]
    slice x3 -> x0, local copies, waits for them, and re-layouts: 46.5 us -> none  [the longest x1 44.6 us: local_step(): out_heads = cross_o[layer].reshape(kv_heads, n_groups, head_dim, width)]
  transfers between devices with their start and end apart: 10 -> 0, of which waited for: 8 -> 0; matrix products, arithmetic and copies ran while one was open for 21% -> 0% of each run, Pallas kernels for 0% -> 0%
where the time goes in v1:
time: 1030 us; the launch traced here: 1010 us
  Pallas kernels  1010 us (98%)
    pallas_call x2, Pallas kernels, post_call(): pl.pallas_call(body, grid=(n_o + n_f + n_d,), in_specs=in_specs, out_spec...  336 us
    pallas_call x2, Pallas kernels, cross_call(): pl.pallas_call(functools.partial(cross_kernel, group, hd, 1024), grid=(gr...  264 us
    pallas_call x2, Pallas kernels, qkv_call(): pl.pallas_call(body, grid=(last + 1,), in_specs=in_specs, out_specs=[pl.B...  209 us
    pallas_call x2, Pallas kernels, self_call(): pl.pallas_call(functools.partial(self_kernel, group, hd), grid=(group + 1...  104 us
    pallas_call x2, Pallas kernels, cross_q_call(): pl.pallas_call(functools.partial(cross_q_kernel, group, layer), grid=(n_o...  95.1 us

profile of v1, /device:TPU:0, one launch (start us, length us, event | category | flops | bytes accessed | tf_op | source)
XLA Modules:
  0.0 1009.9 jit_solution(9288275191897258236)
XLA Ops:
  0.0 132.0 %qkv0.1 = (bf16[3,2048,512]{2,1,0:T(8,128)(2,1)}, bf16[6,1024,256]{2,1,0:T(8,128)(2,1)}, bf16[8,1024,256]{2,1,0:T(8,128)(2,1)}) custom-call(bf16[256,4096]{1,0:T(8,128)(2,1)} %hid.1, bf16[2,4096]{1,0:T(2,128)(2,1)} %refs_1_.3, bf16[2,4096,4096]{2,1,0:T(8,128)(2,1)} %refs_2_.6, bf16[2,4096,4096]{2,1,0:T(8,128)(2,1)} %refs_3_.3, ...), custom_call_target="tpu_custom_call" | custom-call | tf_op jit(solution)/shard_map/qkv0/pallas_call | solution.py:286
  132.0 52.7 %self_attn.2.att = bf16[256,4096]{1,0:T(8,128)(2,1)} custom-call(bf16[3,2048,512]{2,1,0:T(8,128)(2,1)} %get-tuple-element.14.qkv), custom_call_target="tpu_custom_call" | custom-call | tf_op jit(solution)/shard_map/self_attn/pallas_call | solution.py:392
  184.7 45.8 %cross_q0.1 = (bf16[256,4096]{1,0:T(8,128)(2,1)}, bf16[2048,512]{1,0:T(8,128)(2,1)}) custom-call(bf16[256,4096]{1,0:T(8,128)(2,1)} %self_attn.2.att, bf16[256,4096]{1,0:T(8,128)(2,1)} %hid.1, bf16[2,4096]{1,0:T(2,128)(2,1)} %gain.3, bf16[2,4096,4096]{2,1,0:T(8,128)(2,1)} %bitcast.wo, bf16[2,4096,4096]{2,1,0:T(8,128)(2,1)} %wq.3), custom_call_target="tpu_custom_call" | custom-call | tf_op jit(solution)/shard_map/cross_q0/pallas_call | solution.py:543
  231.1 132.4 %cross_attn.2.refs_0_ = bf16[256,4096]{1,0:T(8,128)(2,1)} custom-call(s32[1]{0:T(128)S(6)} %copy.18.mem_len, bf16[2048,512]{1,0:T(8,128)(2,1)} %get-tuple-element.15.q, bf16[6144,256]{1,0:T(8,128)(2,1)} %bitcast.5), custom_call_target="tpu_custom_call" | custom-call | tf_op jit(solution)/shard_map/cross_attn/pallas_call | solution.py:464
  363.6 164.3 %post0.1 = (bf16[256,4096]{1,0:T(8,128)(2,1)}, bf16[6,1024,256]{2,1,0:T(8,128)(2,1)}) custom-call(bf16[256,4096]{1,0:T(8,128)(2,1)} %cross_attn.2.refs_0_, bf16[256,4096]{1,0:T(8,128)(2,1)} %get-tuple-element.17.refs_1_, bf16[2,4096]{1,0:T(2,128)(2,1)} %refs_2_.7, bf16[2,4096,4096]{2,1,0:T(8,128)(2,1)} %bitcast.2.refs_3_, bf16[2,4096,14336]{2,1,0:T(8,128)(2,1)} %refs_4_.7, ...), custom_call_target="tpu_custom_call" | custom-call | tf_op jit(solution)/shard_map/post0/pallas_call | solution.py:686
  527.8 77.4 %qkv1.1.qkv = bf16[3,2048,512]{2,1,0:T(8,128)(2,1)} custom-call(bf16[256,4096]{1,0:T(8,128)(2,1)} %get-tuple-element.19.refs_0_.hid, bf16[2,4096]{1,0:T(2,128)(2,1)} %refs_1_.3, bf16[2,4096,4096]{2,1,0:T(8,128)(2,1)} %refs_2_.6, bf16[2,4096,4096]{2,1,0:T(8,128)(2,1)} %refs_3_.3, bf16[2,4096,4096]{2,1,0:T(8,128)(2,1)} %refs_4_.6), custom_call_target="tpu_custom_call" | custom-call | tf_op jit(solution)/shard_map/qkv1/pallas_call | solution.py:286
  605.2 51.3 %self_attn.3.att = bf16[256,4096]{1,0:T(8,128)(2,1)} custom-call(bf16[3,2048,512]{2,1,0:T(8,128)(2,1)} %qkv1.1.qkv), custom_call_target="tpu_custom_call" | custom-call | tf_op jit(solution)/shard_map/self_attn/pallas_call | solution.py:392
  656.5 49.4 %cross_q1.1 = (bf16[256,4096]{1,0:T(8,128)(2,1)}, bf16[2048,512]{1,0:T(8,128)(2,1)}) custom-call(bf16[256,4096]{1,0:T(8,128)(2,1)} %self_attn.3.att, bf16[256,4096]{1,0:T(8,128)(2,1)} %get-tuple-element.19.refs_0_.hid, bf16[2,4096]{1,0:T(2,128)(2,1)} %gain.3, bf16[2,4096,4096]{2,1,0:T(8,128)(2,1)} %bitcast.wo, bf16[2,4096,4096]{2,1,0:T(8,128)(2,1)} %wq.3), custom_call_target="tpu_custom_call" | custom-call | tf_op jit(solution)/shard_map/cross_q1/pallas_call | solution.py:543
  705.9 131.9 %cross_attn.3.refs_0_ = bf16[256,4096]{1,0:T(8,128)(2,1)} custom-call(s32[1]{0:T(128)S(6)} %copy.18.mem_len, bf16[2048,512]{1,0:T(8,128)(2,1)} %get-tuple-element.20.q, bf16[6144,256]{1,0:T(8,128)(2,1)} %bitcast.4), custom_call_target="tpu_custom_call" | custom-call | tf_op jit(solution)/shard_map/cross_attn/pallas_call | solution.py:464
  837.8 171.6 %post1.1 = bf16[256,4096]{1,0:T(8,128)(2,1)} custom-call(bf16[256,4096]{1,0:T(8,128)(2,1)} %cross_attn.3.refs_0_, bf16[256,4096]{1,0:T(8,128)(2,1)} %get-tuple-element.22.refs_1_, bf16[2,4096]{1,0:T(2,128)(2,1)} %refs_2_.7, bf16[2,4096,4096]{2,1,0:T(8,128)(2,1)} %bitcast.2.refs_3_, bf16[2,4096,14336]{2,1,0:T(8,128)(2,1)} %refs_4_.7, ...), custom_call_target="tpu_custom_call" | custom-call | tf_op jit(solution)/shard_map/post1/pallas_call | solution.py:686

commit v2 on v1

v2 whole, which is shorter than its diff:
```python
import functools

import jax
import jax.numpy as jnp
from jax import lax
from jax.experimental import pallas as pl
from jax.experimental.pallas import tpu as pltpu
from jax.sharding import PartitionSpec as P

EPS = 1e-6
NEG_BIG = -1e30
LOG2E = 1.4426950408889634
MESH = pl.DeviceIdType.MESH
VMEM_LIMIT = 66_000_000
BF16 = jnp.bfloat16
F32 = jnp.float32


def norm_rows(hidden, gain):
    h = hidden.astype(F32)
    inv = lax.rsqrt(jnp.mean(h * h, axis=-1, keepdims=True) + EPS)
    return (h * inv * gain.astype(F32)).astype(BF16)


def dot(a, b):
    return jnp.dot(a, b, preferred_element_type=F32)


def dot_t(a, b):
    return lax.dot_general(a, b, (((1,), (1,)), ((), ())), preferred_element_type=F32)


def params(collective_id, dims=1):
    return pltpu.CompilerParams(
        collective_id=collective_id,
        has_side_effects=collective_id is not None,
        vmem_limit_bytes=VMEM_LIMIT,
        dimension_semantics=("arbitrary",) * dims,
    )


class Exchange:
    def __init__(self, group):
        self.group = group
        self.me = lax.axis_index("sp")
        self.dp = lax.axis_index("dp")

    def peer(self, offset):
        return lax.rem(self.me + offset, self.group)

    def greet(self):
        barrier = pltpu.get_barrier_semaphore()
        for k in range(1, self.group):
            pl.semaphore_signal(
                barrier, inc=1, device_id=(self.dp, self.peer(k)), device_id_type=MESH
            )

    def await_all(self):
        pl.semaphore_wait(pltpu.get_barrier_semaphore(), self.group - 1)

    def copy(self, src, dst, send, recv, target):
        return pltpu.make_async_remote_copy(
            src_ref=src, dst_ref=dst, send_sem=send, recv_sem=recv,
            device_id=(self.dp, target), device_id_type=MESH,
        )


class Stream:
    def __init__(self, ring, sems, phases):
        self.ring, self.sems, self.phases = ring, sems, phases
        self.depth = ring.shape[0]
        self.total = sum(n for n, _ in phases)

    def copies(self, phase, start, step, slot):
        return [
            pltpu.make_async_copy(src, self.ring.at[slot, pl.ds(0, src.shape[0]), cols], self.sems.at[slot, k])
            for k, (src, cols) in enumerate(self.phases[phase][1](step - start))
        ]

    def ranges(self):
        first = 0
        for phase, (n, _) in enumerate(self.phases):
            yield phase, first, first + n
            first += n

    def fetch(self, step):
        slot = lax.rem(step, self.depth)
        for phase, a, b in self.ranges():

            @pl.when((step >= a) & (step < b))
            def _(phase=phase, a=a):
                for cp in self.copies(phase, a, step, slot):
                    cp.start()

    def begin(self, i):
        @pl.when(i == 0)
        def _():
            lax.fori_loop(0, self.depth - 1, lambda k, c: (self.fetch(k), c)[1], 0)

        self.fetch(i + self.depth - 1)
        slot = lax.rem(i, self.depth)
        for phase, a, b in self.ranges():

            @pl.when((i >= a) & (i < b))
            def _(phase=phase, a=a):
                for cp in self.copies(phase, a, i, slot):
                    cp.wait()

        return slot


def cols_at(j, width):
    return pl.ds(pl.multiple_of(j * width, width), width)


def ring_scratch(depth, rows, cols, parts):
    return [pltpu.VMEM((depth, rows, cols), BF16), pltpu.SemaphoreType.DMA((depth, parts))]


def qkv_kernel(group, layer, mem_layers, refs):
    n_w = 3
    it = iter(refs)
    hid, gain = next(it), next(it)
    w = [next(it) for _ in range(n_w)]
    if mem_layers:
        mem, ck, cv = next(it), next(it), next(it)
    out = next(it)
    if mem_layers:
        kv_out, kv_keep = next(it), next(it)
    x, ring, ring_sem, buf, ssem, rsem, lsem = (next(it) for _ in range(7))
    if mem_layers:
        mem_v, kv_buf, kvs, kvr, kvl, keep_sem, mem_sem = (next(it) for _ in range(7))
    ex = Exchange(group)
    me = ex.me
    i = pl.program_id(0)
    rows = hid.shape[0]
    width = buf.shape[2]
    n_q = n_w * group
    pairs = group // 2

    phases = [(group, lambda j, t=t: [(w[t].at[layer, :, cols_at(ex.peer(j + 1), width)], slice(0, width))]) for t in range(n_w)]
    if mem_layers:
        hd2 = width // 2
        phases.append((
            mem_layers * pairs,
            lambda j: [
                (c.at[lax.div(j, pairs), :, cols_at(lax.rem(j, pairs), hd2)], slice(k * hd2, (k + 1) * hd2))
                for k, c in enumerate((ck, cv))
            ],
        ))
    stream = Stream(ring, ring_sem, phases)
    last = stream.total

    @pl.when(i == 0)
    def _():
        ex.greet()
        if mem_layers:
            pltpu.make_async_copy(mem, mem_v, mem_sem).start()

    slot = stream.begin(i)

    @pl.when(i == 0)
    def _():
        x[...] = norm_rows(hid[...], gain[layer : layer + 1, :])

    @pl.when(i == 1)
    def _():
        ex.await_all()

    def out_at(t, p):
        return out.at[t, pl.ds(pl.multiple_of(p * rows, rows), rows)]

    def own_copy(t):
        return pltpu.make_async_copy(buf.at[t * group + group - 1], out_at(t, me), lsem.at[t])

    @pl.when((i >= 1) & (i <= n_q))
    def _():
        b = i - 1
        t, r = lax.div(b, group), lax.rem(b, group)

        @pl.when(r < group - 1)
        def _():
            ex.copy(buf.at[b], out_at(t, me), ssem.at[b], rsem.at[t, me], ex.peer(r + 1)).start()

        @pl.when(r == group - 1)
        def _():
            own_copy(t).start()

    @pl.when(i < n_q)
    def _():
        buf[i] = dot(x[...], ring[slot]).astype(BF16)

    if mem_layers:
        hd = width // 4
        mem_rows = mem.shape[0]
        senders = kv_out.shape[0]

        @pl.when(i == n_q)
        def _():
            pltpu.make_async_copy(mem, mem_v, mem_sem).wait()

        def kv_copy(d):
            return ex.copy(kv_buf.at[0, d], kv_out.at[me], kvs.at[d], kvr.at[me], d)

        keep_copy = pltpu.make_async_copy(kv_buf.at[1], kv_keep, keep_sem)

        @pl.when((i > n_q) & (i <= n_q + pairs) & (me < senders))
        def _():
            for side in range(2):
                d = 2 * (i - n_q - 1) + side

                @pl.when(d != me)
                def _():
                    kv_copy(d).start()

                @pl.when(d == me)
                def _():
                    pltpu.make_async_copy(kv_buf.at[0, d], kv_out.at[me], kvl).start()

        @pl.when((i >= n_q) & (i < last) & (me < senders))
        def _():
            j = i - n_q
            m, pair = lax.div(j, pairs), lax.rem(j, pairs)
            for c in range(4):
                rs = slice(c * mem_rows // 4, (c + 1) * mem_rows // 4)
                res = dot(mem_v[rs, :], ring[slot]).astype(BF16)
                for side in range(2):
                    kv_buf[m, 2 * pair + side, rs, 0:hd] = res[:, side * hd : (side + 1) * hd]
                    kv_buf[m, 2 * pair + side, rs, hd : 2 * hd] = res[:, (2 + side) * hd : (3 + side) * hd]

        @pl.when((i == last) & (me < senders))
        def _():
            keep_copy.start()

    @pl.when(i == last)
    def _():
        for t in range(n_w):
            own_copy(t).wait()
            for k in range(1, group):
                p = ex.peer(k)
                ex.copy(buf.at[0], out_at(t, p), ssem.at[t * group + k - 1], rsem.at[t, p], p).wait()
        if mem_layers:

            @pl.when(me < senders)
            def _():
                pltpu.make_async_copy(kv_buf.at[0, 0], kv_out.at[me], kvl).wait()
                for k in range(1, group):
                    kv_copy(ex.peer(k)).wait_send()
                keep_copy.wait()

            for p in range(senders):

                @pl.when(me != p)
                def _(p=p):
                    ex.copy(kv_buf.at[0, 0], kv_out.at[p], kvs.at[0], kvr.at[p], p).wait_recv()


ANY = pl.BlockSpec(memory_space=pl.ANY)


def held(shape):
    return pl.BlockSpec(shape, lambda i: (0,) * len(shape), pipeline_mode=pl.Buffered(1))


def qkv_call(mesh, layer, hidden, gain, ws, mem=None, ck=None, cv=None):
    group = mesh.shape["sp"]
    rows, width = hidden.shape
    per_dev = ws[0].shape[2] // group
    steps = 3 * group
    mem_layers = 0 if mem is None else ck.shape[0]
    in_specs = [held((rows, width)), held(gain.shape)] + [ANY] * 3
    args = [hidden, gain, *ws]
    out_shape = [jax.ShapeDtypeStruct((3, rows * group, per_dev), BF16)]
    scratch = [pltpu.VMEM((rows, width), BF16)] + ring_scratch(4, width, per_dev, 2) + [
        pltpu.VMEM((3 * group, rows, per_dev), BF16),
        pltpu.SemaphoreType.DMA((3 * group,)),
        pltpu.SemaphoreType.DMA((3, group)),
        pltpu.SemaphoreType.DMA((3,)),
    ]
    if mem_layers:
        mem_rows = mem.shape[0]
        hd = ck.shape[2] // group
        senders = group * 3 // 4
        in_specs += [ANY] * 3
        args += [mem, ck, cv]
        out_shape += [
            jax.ShapeDtypeStruct((senders, mem_rows, 2 * hd), BF16),
            jax.ShapeDtypeStruct((group, mem_rows, 2 * hd), BF16),
        ]
        scratch += [
            pltpu.VMEM((mem_rows, width), BF16),
            pltpu.VMEM((2, group, mem_rows, 2 * hd), BF16),
            pltpu.SemaphoreType.DMA((group,)),
            pltpu.SemaphoreType.DMA((group,)),
            pltpu.SemaphoreType.DMA,
            pltpu.SemaphoreType.DMA,
            pltpu.SemaphoreType.DMA,
        ]
        steps += mem_layers * group // 2

    def body(*refs):
        qkv_kernel(group, layer, mem_layers, refs)

    return pl.pallas_call(
        body,
        grid=(steps + 1,),
        in_specs=in_specs,
        out_specs=[ANY] * len(out_shape),
        out_shape=out_shape,
        scratch_shapes=scratch,
        compiler_params=params(layer),
        name=f"qkv{layer}",
    )(*args)


def send_back(ex, i, group, rows, cols, buf, out, ssem, rsem, lsem):
    me = ex.me

    def out_at(p):
        return out.at[:, pl.ds(pl.multiple_of(p * cols, cols), cols)]

    own = pltpu.make_async_copy(buf.at[group - 1], out_at(me), lsem)

    @pl.when((i >= 1) & (i < group))
    def _():
        r = i - 1
        ex.copy(buf.at[r], out_at(me), ssem.at[r], rsem.at[me], ex.peer(r + 1)).start()

    @pl.when(i == group)
    def _():
        own.start()
        for k in range(1, group):
            p = ex.peer(k)
            ex.copy(buf.at[k - 1], out_at(p), ssem.at[k - 1], rsem.at[p], p).wait()
        own.wait()


def back_scratch(group, rows, cols):
    return [
        pltpu.VMEM((group, rows, cols), BF16),
        pltpu.SemaphoreType.DMA((group,)),
        pltpu.SemaphoreType.DMA((group,)),
        pltpu.SemaphoreType.DMA,
    ]


def soft_start(heads, rows, hd):
    return tuple(
        (jnp.full((1, rows), NEG_BIG, F32), jnp.zeros((1, rows), F32), jnp.zeros((hd, rows), F32))
        for _ in range(heads)
    )


def soft_block(carry, scores, ahead, values, coef, ss):
    heads = len(carry)
    out = []
    late = None

    def land(late):
        m, l, acc, alpha, p, h = late
        out.append((m, l, acc * alpha + dot(values(h), p)))

    for h in range(heads):
        s = ss[h % 2]
        coming = scores(h + 1) if h + 1 < heads else ahead()
        m_old, l, acc = carry[h]
        m_new = jnp.maximum(m_old, jnp.max(s, axis=0, keepdims=True))
        p = jnp.exp2((s - m_new) * coef)
        alpha = jnp.exp2((m_old - m_new) * coef)
        l_new = l * alpha + jnp.sum(p, axis=0, keepdims=True)
        p = p.astype(BF16)
        if late is not None:
            land(late)
        if coming is not None:
            ss[(h + 1) % 2] = coming
        late = (m_new, l_new, acc, alpha, p, h)
    land(late)
    return tuple(out)


def soft_finish(carry, hd, buf, i):
    for h, (_, l, acc) in enumerate(carry):
        buf[i, :, h * hd : (h + 1) * hd] = (acc / l).T.astype(BF16)


def self_kernel(group, hd, qkv, out, buf, ssem, rsem, lsem, vt, ss):
    ex = Exchange(group)
    i = pl.program_id(0)
    rows, cols = buf.shape[1], buf.shape[2]
    heads = cols // hd
    bk = 2 * rows
    coef = hd**-0.5 * LOG2E

    @pl.when(i == 0)
    def _():
        ex.greet()
        for c in range(qkv.shape[1] // bk):
            cs = slice(c * bk, (c + 1) * bk)
            vt[:, cs] = qkv[2, cs, :].astype(F32).T.astype(BF16)

    @pl.when(i == 1)
    def _():
        ex.await_all()

    @pl.when(i < group)
    def _():
        d = ex.peer(i + 1)
        r0 = pl.multiple_of(d * rows, rows)

        def heads_of(h):
            return slice(h * hd, (h + 1) * hd)

        def step(kb, carry, masked):
            k0 = pl.multiple_of(kb * bk, bk)

            def scores(h, k0=k0):
                s = dot_t(qkv[1, pl.ds(k0, bk), heads_of(h)], qkv[0, pl.ds(r0, rows), heads_of(h)])
                return jnp.where(allowed, s, NEG_BIG) if masked else s

            if masked:
                col = k0 + lax.broadcasted_iota(jnp.int32, (bk, rows), 0)
                row = r0 + lax.broadcasted_iota(jnp.int32, (bk, rows), 1)
                allowed = row >= col
            ss[0] = scores(0)
            return soft_block(carry, scores, lambda: None, lambda h: vt[heads_of(h), pl.ds(k0, bk)], coef, ss)

        full = lax.div(d, 2)
        carry = lax.fori_loop(0, full, lambda kb, c: step(kb, c, False), soft_start(heads, rows, hd))
        carry = step(full, carry, True)
        soft_finish(carry, hd, buf, i)

    send_back(ex, i, group, rows, cols, buf, out, ssem, rsem, lsem)


def self_call(mesh, hd, qkv, cid):
    group = mesh.shape["sp"]
    _, all_rows, cols = qkv.shape
    rows = all_rows // group
    return pl.pallas_call(
        functools.partial(self_kernel, group, hd),
        grid=(group + 1,),
        in_specs=[held(qkv.shape)],
        out_specs=ANY,
        out_shape=jax.ShapeDtypeStruct((rows, cols * group), BF16),
        scratch_shapes=back_scratch(group, rows, cols)
        + [pltpu.VMEM((cols, all_rows), BF16), pltpu.VMEM((2, 2 * rows, rows), F32)],
        compiler_params=params(cid),
        name="self_attn",
    )(qkv)


def cross_kernel(group, hd, bk, mem_len, q, kv, out, buf, ssem, rsem, lsem, keys, vt, qa, ss):
    ex = Exchange(group)
    i = pl.program_id(0)
    rows, cols = buf.shape[1], buf.shape[2]
    heads = cols // hd
    coef = hd**-0.5 * LOG2E
    n_kb = kv.shape[0] // bk

    @pl.when(i == 0)
    def _():
        ex.greet()
        first = lax.broadcasted_iota(jnp.int32, (bk, hd), 1) == 0
        for c in range(n_kb):
            cs = slice(c * bk, (c + 1) * bk)
            pos = c * bk + lax.broadcasted_iota(jnp.int32, (bk, hd), 0)
            keys[cs, 0:hd] = kv[cs, 0:hd]
            keys[cs, hd : 2 * hd] = jnp.where(first & (pos >= mem_len[0]), NEG_BIG, 0.0).astype(BF16)
            vt[:, cs] = kv[cs, hd : 2 * hd].astype(F32).T.astype(BF16)
        for h in range(heads):
            one = lax.broadcasted_iota(jnp.int32, (rows, hd), 1) == 0
            qa[h, :, hd : 2 * hd] = jnp.where(one, 1.0, 0.0).astype(BF16)

    @pl.when(i == 1)
    def _():
        ex.await_all()

    @pl.when(i < group)
    def _():
        r0 = pl.multiple_of(ex.peer(i + 1) * rows, rows)
        for h in range(heads):
            qa[h, :, 0:hd] = q[pl.ds(r0, rows), h * hd : (h + 1) * hd]
        ss[0] = dot_t(keys[0:bk, :], qa[0])

        def step(kb, carry):
            k0 = pl.multiple_of(kb * bk, bk)
            after = pl.multiple_of(jnp.minimum(k0 + bk, (n_kb - 1) * bk), bk)
            return soft_block(
                carry,
                lambda h: dot_t(keys[pl.ds(k0, bk), :], qa[h]),
                lambda: dot_t(keys[pl.ds(after, bk), :], qa[0]),
                lambda h: vt[:, pl.ds(k0, bk)],
                coef,
                ss,
            )

        soft_finish(lax.fori_loop(0, n_kb, step, soft_start(heads, rows, hd)), hd, buf, i)

    send_back(ex, i, group, rows, cols, buf, out, ssem, rsem, lsem)


def cross_call(mesh, hd, mem_len, q, kv, cid, used, bk):
    group = mesh.shape["sp"]
    all_rows, cols = q.shape
    rows = all_rows // group
    heads = cols // hd
    return pl.pallas_call(
        functools.partial(cross_kernel, group, hd, bk),
        grid=(group + 1,),
        in_specs=[pl.BlockSpec(memory_space=pltpu.SMEM), held(q.shape), held((used, 2 * hd))],
        out_specs=ANY,
        out_shape=jax.ShapeDtypeStruct((rows, cols * group), BF16),
        scratch_shapes=back_scratch(group, rows, cols)
        + [
            pltpu.VMEM((used, 2 * hd), BF16),
            pltpu.VMEM((hd, used), BF16),
            pltpu.VMEM((heads, rows, 2 * hd), BF16),
            pltpu.VMEM((2, bk, rows), F32),
        ],
        compiler_params=params(cid),
        name=f"cross_attn{used}",
    )(mem_len, q, kv)


LENGTHS = ((3072, 1536), (4096, 2048), (5120, 2560), (6144, 2048))


def cross_any(mesh, hd, mem_len, q, kv, cid):
    index = sum((mem_len[0] > used).astype(jnp.int32) for used, _ in LENGTHS[:-1])
    branches = [
        functools.partial(lambda used, bk, cid, m, a, b: cross_call(mesh, hd, m, a, b, cid, used, bk), used, bk, cid + n)
        for n, (used, bk) in enumerate(LENGTHS)
    ]
    return lax.switch(index, branches, mem_len, q, kv)


def cross_q_kernel(group, layer, att, hid, gain, wo, wq, out, q_out, x, ring, ring_sem, buf, ssem, rsem, lsem):
    ex = Exchange(group)
    me = ex.me
    i = pl.program_id(0)
    rows = hid.shape[0]
    tn = ring.shape[2]
    n_o = hid.shape[1] // tn

    @pl.when(i == 0)
    def _():
        ex.greet()

    stream = Stream(ring, ring_sem, [
        (n_o, lambda j: [(wo.at[layer, :, cols_at(j, tn)], slice(0, tn))]),
        (group, lambda j: [(wq.at[layer, :, cols_at(ex.peer(j + 1), tn)], slice(0, tn))]),
    ])
    slot = stream.begin(i)

    @pl.when(i < n_o)
    def _():
        cs = cols_at(i, tn)
        out[:, cs] = (hid[:, cs].astype(F32) + dot(att[...], ring[slot])).astype(BF16)

    @pl.when(i == n_o)
    def _():
        ex.await_all()
        x[...] = norm_rows(out[...], gain[layer : layer + 1, :])

    def out_at(p):
        return q_out.at[pl.ds(pl.multiple_of(p * rows, rows), rows)]

    own = pltpu.make_async_copy(buf.at[group - 1], out_at(me), lsem)

    @pl.when((i > n_o) & (i < n_o + group))
    def _():
        r = i - n_o - 1
        ex.copy(buf.at[r], out_at(me), ssem.at[r], rsem.at[me], ex.peer(r + 1)).start()

    @pl.when((i >= n_o) & (i < n_o + group))
    def _():
        buf[i - n_o] = dot(x[...], ring[slot]).astype(BF16)

    @pl.when(i == n_o + group)
    def _():
        own.start()
        for k in range(1, group):
            p = ex.peer(k)
            ex.copy(buf.at[k - 1], out_at(p), ssem.at[k - 1], rsem.at[p], p).wait()
        own.wait()


def cross_q_call(mesh, layer, att, hidden, gain, wo, wq, cid):
    group = mesh.shape["sp"]
    rows, width = hidden.shape
    tn = wq.shape[2] // group
    n_o = width // tn
    return pl.pallas_call(
        functools.partial(cross_q_kernel, group, layer),
        grid=(n_o + group + 1,),
        in_specs=[held((rows, width)), held((rows, width)), held(gain.shape), ANY, ANY],
        out_specs=[held((rows, width)), ANY],
        out_shape=[
            jax.ShapeDtypeStruct((rows, width), BF16),
            jax.ShapeDtypeStruct((rows * group, tn), BF16),
        ],
        scratch_shapes=[pltpu.VMEM((rows, width), BF16)]
        + ring_scratch(5, width, tn, 1)
        + back_scratch(group, rows, tn),
        compiler_params=params(cid),
        name=f"cross_q{layer}",
    )(att, hidden, gain, wo, wq)


def post_kernel(group, layer, senders, refs):
    it = iter(refs)
    att, hid, gain, wo, wg, wu, wd = (next(it) for _ in range(7))
    keep = next(it) if senders else None
    out = next(it)
    kv_out = next(it) if senders else None
    y, x, act, acc, ring, ring_sem = (next(it) for _ in range(6))
    i = pl.program_id(0)
    width = hid.shape[1]
    ff = act.shape[1]
    tn = ring.shape[2]
    tf = tn // 2
    parts = 4
    tk = ff // parts
    n_o, n_f, n_d = width // tn, ff // tf, width // tn * parts
    last = n_o + n_f + n_d - 1
    if senders:
        kvs, kvr, kvl = (next(it) for _ in range(3))
        ex = Exchange(group)
        me = ex.me

        def kv_copy(d):
            return ex.copy(keep.at[d], kv_out.at[me], kvs.at[d], kvr.at[me], d)

        own = pltpu.make_async_copy(keep.at[me], kv_out.at[me], kvl)

        @pl.when(i == 0)
        def _():
            ex.greet()

    stream = Stream(ring, ring_sem, [
        (n_o, lambda j: [(wo.at[layer, :, cols_at(j, tn)], slice(0, tn))]),
        (n_f, lambda j: [
            (wg.at[layer, :, cols_at(j, tf)], slice(0, tf)),
            (wu.at[layer, :, cols_at(j, tf)], slice(tf, tn)),
        ]),
        (n_d, lambda j: [(
            wd.at[layer, pl.ds(pl.multiple_of(lax.rem(j, parts) * tk, tk), tk), cols_at(lax.div(j, parts), tn)],
            slice(0, tn),
        )]),
    ])
    slot = stream.begin(i)

    if senders:

        @pl.when(i == 1)
        def _():
            ex.await_all()

        @pl.when((i == 1) & (me < senders))
        def _():
            own.start()
            for k in range(1, group):
                kv_copy(ex.peer(k)).start()

    @pl.when(i < n_o)
    def _():
        cs = cols_at(i, tn)
        y[:, cs] = (hid[:, cs].astype(F32) + dot(att[...], ring[slot])).astype(BF16)

    @pl.when(i == n_o)
    def _():
        x[...] = norm_rows(y[...], gain[layer : layer + 1, :])

    @pl.when((i >= n_o) & (i < n_o + n_f))
    def _():
        g = dot(x[...], ring[slot, :, 0:tf])
        u = dot(x[...], ring[slot, :, tf:tn])
        act[:, cols_at(i - n_o, tf)] = (g * jax.nn.sigmoid(g) * u).astype(BF16)

    @pl.when(i >= n_o + n_f)
    def _():
        j = i - n_o - n_f
        part, block = lax.rem(j, parts), lax.div(j, parts)
        prod = dot(act[:, pl.ds(pl.multiple_of(part * tk, tf), tk)], ring[slot, 0:tk, :])

        @pl.when(part == 0)
        def _():
            acc[...] = prod

        @pl.when(part > 0)
        def _():
            acc[...] += prod

        @pl.when(part == parts - 1)
        def _():
            cs = cols_at(block, tn)
            out[:, cs] = (y[:, cs].astype(F32) + acc[...]).astype(BF16)

    if senders:

        @pl.when(i == last)
        def _():
            @pl.when(me < senders)
            def _():
                own.wait()
                for k in range(1, group):
                    kv_copy(ex.peer(k)).wait_send()

            for p in range(senders):

                @pl.when(me != p)
                def _(p=p):
                    ex.copy(keep.at[p], kv_out.at[p], kvs.at[0], kvr.at[p], p).wait_recv()


def post_call(mesh, layer, att, hidden, gain, wo, wg, wu, wd, keep, cid):
    group = mesh.shape["sp"]
    rows, width = hidden.shape
    ff = wg.shape[2]
    tn = 1024
    senders = 0 if keep is None else group * 3 // 4
    in_specs = [held((rows, width)), held((rows, width)), held(gain.shape)] + [ANY] * 4
    args = [att, hidden, gain, wo, wg, wu, wd]
    out_specs = [held((rows, width))]
    out_shape = [jax.ShapeDtypeStruct((rows, width), BF16)]
    scratch = [
        pltpu.VMEM((rows, width), BF16),
        pltpu.VMEM((rows, width), BF16),
        pltpu.VMEM((rows, ff), BF16),
        pltpu.VMEM((rows, tn), F32),
    ] + ring_scratch(3, width, tn, 2)
    if senders:
        in_specs.append(ANY)
        args.append(keep)
        out_specs.append(ANY)
        out_shape.append(jax.ShapeDtypeStruct((senders,) + keep.shape[1:], BF16))
        scratch += [
            pltpu.SemaphoreType.DMA((group,)),
            pltpu.SemaphoreType.DMA((group,)),
            pltpu.SemaphoreType.DMA,
        ]

    def body(*refs):
        post_kernel(group, layer, senders, refs)

    return pl.pallas_call(
        body,
        grid=(width // tn + ff // (tn // 2) + width // tn * 4,),
        in_specs=in_specs,
        out_specs=out_specs,
        out_shape=out_shape,
        scratch_shapes=scratch,
        compiler_params=params(cid if senders else None),
        name=f"post{layer}",
    )(*args)


def solution(mesh):
    row_spec = P(("dp", "sp"), None)

    def local_step(hidden, memory, mem_len, norm_self, norm_cross, norm_mlp, self_q, self_k, self_v, self_o, cross_q, cross_k, cross_v, cross_o, mlp_gate, mlp_up, mlp_down):
        layers, _, hd, width = self_o.shape
        self_o = self_o.reshape(layers, -1, width)
        cross_o = cross_o.reshape(layers, -1, width)
        keep = None
        for layer in range(layers):
            if layer == 0:
                qkv, kv, keep = qkv_call(mesh, layer, hidden, norm_self, (self_q, self_k, self_v), memory, cross_k, cross_v)
            else:
                (qkv,) = qkv_call(mesh, layer, hidden, norm_self, (self_q, self_k, self_v))
            att = self_call(mesh, hd, qkv, layers)
            hidden, q = cross_q_call(mesh, layer, att, hidden, norm_cross, self_o, cross_q, layers + 1 + layer)
            att = cross_any(mesh, hd, mem_len, q, kv.reshape(-1, 2 * hd), 2 * layers + 2)
            res = post_call(mesh, layer, att, hidden, norm_mlp, cross_o, mlp_gate, mlp_up, mlp_down, keep, 2 * layers + 1)
            hidden = res[0]
            if layer == 0:
                kv, keep = res[1], None
        return hidden

    return jax.shard_map(local_step, mesh=mesh, in_specs=(row_spec, row_spec, P("dp")) + (P(),) * 14, out_specs=row_spec, check_vma=False)
```

time: 1030 us -> 749 us (0.73)
  Pallas kernels: 1010 us -> 723 us
  loops' own time: 0 us -> 13.6 us
    pallas_call x6, Pallas kernels: 810 us -> 556 us  [the longest x2 246 us: post_call(): pl.pallas_call(body, grid=(width // tn + ff // (tn // 2) + width // tn *...]
    pallas_call x2, Pallas kernels: 104 us -> 77.7 us  [self_call(): pl.pallas_call(functools.partial(self_kernel, group, hd), grid=(group + 1...]
    another operation x0 -> x2, loops' own time: none -> 13.6 us  [cross_any(): return lax.switch(index, branches, mem_len, q, kv)]
where the time goes in v2:
time: 749 us; the launch traced here: 738 us
  Pallas kernels  723 us (97%)
  loops' own time  13.6 us (2%)
    pallas_call x2, Pallas kernels, post_call(): pl.pallas_call(body, grid=(width // tn + ff // (tn // 2) + width // tn *...  246 us
    pallas_call x2, Pallas kernels, qkv_call(): pl.pallas_call(body, grid=(steps + 1,), in_specs=in_specs, out_specs=[ANY...  203 us
    pallas_call x2, Pallas kernels, cross_call(): pl.pallas_call(functools.partial(cross_kernel, group, hd, bk), grid=(grou...  107 us
    pallas_call x2, Pallas kernels, cross_q_call(): pl.pallas_call(functools.partial(cross_q_kernel, group, layer), grid=(n_o...  89.3 us
    pallas_call x2, Pallas kernels, self_call(): pl.pallas_call(functools.partial(self_kernel, group, hd), grid=(group + 1...  77.7 us

profile of v2, /device:TPU:0, one launch (start us, length us, event | category | flops | bytes accessed | tf_op | source)
XLA Modules:
  0.0 737.7 jit_solution(17972449035585544587)
XLA Ops:
  0.7 123.4 %qkv0.1 = (bf16[3,2048,512]{2,1,0:T(8,128)(2,1)}, bf16[6,1024,256]{2,1,0:T(8,128)(2,1)}, bf16[8,1024,256]{2,1,0:T(8,128)(2,1)}) custom-call(bf16[256,4096]{1,0:T(8,128)(2,1)} %hid.1, bf16[2,4096]{1,0:T(2,128)(2,1)} %refs_1_.3, bf16[2,4096,4096]{2,1,0:T(8,128)(2,1)} %refs_2_.6, bf16[2,4096,4096]{2,1,0:T(8,128)(2,1)} %refs_3_.3, ...), custom_call_target="tpu_custom_call" | custom-call | tf_op jit(solution)/shard_map/qkv0/pallas_call | solution.py:304
  124.1 39.5 %self_attn.2.att = bf16[256,4096]{1,0:T(8,128)(2,1)} custom-call(bf16[3,2048,512]{2,1,0:T(8,128)(2,1)} %get-tuple-element.96.qkv), custom_call_target="tpu_custom_call" | custom-call | tf_op jit(solution)/shard_map/self_attn/pallas_call | solution.py:439
  163.6 43.5 %cross_q0.1 = (bf16[256,4096]{1,0:T(8,128)(2,1)}, bf16[2048,512]{1,0:T(8,128)(2,1)}) custom-call(bf16[256,4096]{1,0:T(8,128)(2,1)} %self_attn.2.att, bf16[256,4096]{1,0:T(8,128)(2,1)} %hid.1, bf16[2,4096]{1,0:T(2,128)(2,1)} %gain.3, bf16[2,4096,4096]{2,1,0:T(8,128)(2,1)} %bitcast.1.wo, bf16[2,4096,4096]{2,1,0:T(8,128)(2,1)} %wq.3), custom_call_target="tpu_custom_call" | custom-call | tf_op jit(solution)/shard_map/cross_q0/pallas_call | solution.py:593
  207.1 61.9 %conditional.2 = (bf16[256,4096]{1,0:T(8,128)(2,1)}) conditional(s32[]{:T(128)} %bitcast, (s32[1]{0:T(128)}, bf16[2048,512]{1,0:T(8,128)(2,1)}, bf16[6144,256]{1,0:T(8,128)(2,1)}) %tuple.43, (s32[1]{0:T(128)}, bf16[2048,512]{1,0:T(8,128)(2,1)}, bf16[6144,256]{1,0:T(8,128)(2,1)}) %tuple.44, (s32[1]{0:T(128)}, ...), branch_computations={%region_0.0_spmd, %region_1.0_spmd, %region_2.0_spmd, %region_3.0_... | conditional | bytes 8 | solution.py:534
  207.4 53.2 %cross_attn4096.2 = bf16[256,4096]{1,0:T(8,128)(2,1)} custom-call(s32[1]{0:T(128)} %get-tuple-element.64.mem_len, bf16[2048,512]{1,0:T(8,128)(2,1)} %get-tuple-element.66.q, bf16[6144,256]{1,0:T(8,128)(2,1)} %get-tuple-element.68.kv), custom_call_target="tpu_custom_call" | custom-call | tf_op jit(solution)/shard_map/cond/branch_1_fun/cross_attn4096/pallas_call | solution.py:507
  269.1 124.3 %post0.1 = (bf16[256,4096]{1,0:T(8,128)(2,1)}, bf16[6,1024,256]{2,1,0:T(8,128)(2,1)}) custom-call(bf16[256,4096]{1,0:T(8,128)(2,1)} %get-tuple-element.105.refs_0_, bf16[256,4096]{1,0:T(8,128)(2,1)} %get-tuple-element.99.refs_1_, bf16[2,4096]{1,0:T(2,128)(2,1)} %refs_2_.7, bf16[2,4096,4096]{2,1,0:T(8,128)(2,1)} %bitcast.3.refs_3_, ...), custom_call_target="tpu_custom_call" | custom-call | tf_op jit(solution)/shard_map/post0/pallas_call | solution.py:746
  393.4 79.9 %qkv1.1.qkv = bf16[3,2048,512]{2,1,0:T(8,128)(2,1)} custom-call(bf16[256,4096]{1,0:T(8,128)(2,1)} %get-tuple-element.101.refs_0_.hid, bf16[2,4096]{1,0:T(2,128)(2,1)} %refs_1_.3, bf16[2,4096,4096]{2,1,0:T(8,128)(2,1)} %refs_2_.6, bf16[2,4096,4096]{2,1,0:T(8,128)(2,1)} %refs_3_.3, bf16[2,4096,4096]{2,1,0:T(8,128)(2,1)} %refs_4_.6), custom_call_target="tpu_custom_call" | custom-call | tf_op jit(solution)/shard_map/qkv1/pallas_call | solution.py:304
  473.2 38.2 %self_attn.3.att = bf16[256,4096]{1,0:T(8,128)(2,1)} custom-call(bf16[3,2048,512]{2,1,0:T(8,128)(2,1)} %qkv1.1.qkv), custom_call_target="tpu_custom_call" | custom-call | tf_op jit(solution)/shard_map/self_attn/pallas_call | solution.py:439
  511.5 45.7 %cross_q1.1 = (bf16[256,4096]{1,0:T(8,128)(2,1)}, bf16[2048,512]{1,0:T(8,128)(2,1)}) custom-call(bf16[256,4096]{1,0:T(8,128)(2,1)} %self_attn.3.att, bf16[256,4096]{1,0:T(8,128)(2,1)} %get-tuple-element.101.refs_0_.hid, bf16[2,4096]{1,0:T(2,128)(2,1)} %gain.3, bf16[2,4096,4096]{2,1,0:T(8,128)(2,1)} %bitcast.1.wo, bf16[2,4096,4096]{2,1,0:T(8,128)(2,1)} %wq.3), custom_call_target="tpu_custom_call" | custom-call | tf_op jit(solution)/shard_map/cross_q1/pallas_call | solution.py:593
  557.2 58.3 %conditional.3 = (bf16[256,4096]{1,0:T(8,128)(2,1)}) conditional(s32[]{:T(128)} %bitcast, (s32[1]{0:T(128)}, bf16[2048,512]{1,0:T(8,128)(2,1)}, bf16[6144,256]{1,0:T(8,128)(2,1)}) %tuple.39, (s32[1]{0:T(128)}, bf16[2048,512]{1,0:T(8,128)(2,1)}, bf16[6144,256]{1,0:T(8,128)(2,1)}) %tuple.40, (s32[1]{0:T(128)}, ...), branch_computations={%region_4.0_spmd, %region_5.0_spmd, %region_6.0_spmd, %region_7.0_... | conditional | bytes 8 | solution.py:534
  557.2 53.4 %cross_attn4096.3 = bf16[256,4096]{1,0:T(8,128)(2,1)} custom-call(s32[1]{0:T(128)} %get-tuple-element.78.mem_len, bf16[2048,512]{1,0:T(8,128)(2,1)} %get-tuple-element.79.q, bf16[6144,256]{1,0:T(8,128)(2,1)} %get-tuple-element.80.kv), custom_call_target="tpu_custom_call" | custom-call | tf_op jit(solution)/shard_map/cond/branch_1_fun/cross_attn4096/pallas_call | solution.py:507
  615.5 121.7 %post1.1 = bf16[256,4096]{1,0:T(8,128)(2,1)} custom-call(bf16[256,4096]{1,0:T(8,128)(2,1)} %get-tuple-element.106.refs_0_, bf16[256,4096]{1,0:T(8,128)(2,1)} %get-tuple-element.104.refs_1_, bf16[2,4096]{1,0:T(2,128)(2,1)} %refs_2_.7, bf16[2,4096,4096]{2,1,0:T(8,128)(2,1)} %bitcast.3.refs_3_, bf16[2,4096,14336]{2,1,0:T(8,128)(2,1)} %refs_4_.7, ...), custom_call_target="tpu_custom_call" | custom-call | tf_op jit(solution)/shard_map/post1/pallas_call | solution.py:746
